TPU v7x, 256 devices: a whole 4x4x8 slice. The times are simulated.
256 devices in a mesh: leaf: 64 (over y, z, core), grid: 4 (over x).
Axes of the slice: x: 4, y: 4, z: 8, core: 2. Of those that a mesh axis runs over, the one named last changes fastest.
Arguments:
- source_leaf: float32 [8, 32768], P(None, ('leaf', 'grid')), may hold values from -6 to 6
- block_leaf: float32 [32768, 128], P(('leaf', 'grid')), may hold values from -0.5 to 0.5
- expand_leaf: float32 [32768, 128], P(('leaf', 'grid')), may hold values from -0.5 to 0.5
- basis_leaf: float32 [32768, 256], P(('leaf', 'grid')), may hold values from -0.25 to 0.25
- pivot_leaf: float32 [32768], P(('leaf', 'grid')), may hold values from -2 to 2
- couple_leaf: float32 [65536, 128], P(('leaf', 'grid')), may hold values from -0.5 to 0.5
- ranks_leaf: int32 [64, 2], replicated, may hold values from 32 to 128
- targets_leaf: int32 [65536], P(('leaf', 'grid')), may hold values from 0 to 16383, as said below
- source_middle: float32 [8, 32768], P(None, ('leaf', 'grid')), may hold values from -6 to 6
- block_middle: float32 [32768, 128], P(('leaf', 'grid')), may hold values from -0.5 to 0.5
- expand_middle: float32 [32768, 128], P(('leaf', 'grid')), may hold values from -0.5 to 0.5
- basis_middle: float32 [32768, 256], P(('leaf', 'grid')), may hold values from -0.0625 to 0.0625
- pivot_middle: float32 [32768], P(('leaf', 'grid')), may hold values from -2 to 2
- couple_middle: float32 [32768, 128], P(('leaf', 'grid')), may hold values from -0.5 to 0.5
- ranks_middle: int32 [4, 2], replicated, may hold values from 32 to 128
- targets_middle: int32 [32768], P(('leaf', 'grid')), may hold values from 0 to 32767, as said below
- source_upper: float32 [8, 32768], P(None, ('leaf', 'grid')), may hold values from -6 to 6
- block_upper: float32 [32768, 128], P(('leaf', 'grid')), may hold values from -0.5 to 0.5
- expand_upper: float32 [32768, 128], P(('leaf', 'grid')), may hold values from -0.5 to 0.5
- basis_upper: float32 [32768, 256], P(('leaf', 'grid')), may hold values from -0.046875 to 0.046875
- pivot_upper: float32 [32768], P(('leaf', 'grid')), may hold values from -2 to 2
- couple_upper: float32 [32768, 128], P(('leaf', 'grid')), may hold values from -0.5 to 0.5
- ranks_upper: int32 [2, 2], replicated, may hold values from 32 to 128
- targets_upper: int32 [32768], P(('leaf', 'grid')), may hold values from 0 to 32767, as said below
- source_root: float32 [8, 32768], P(None, ('leaf', 'grid')), may hold values from -6 to 6
- block_root: float32 [32768, 128], P(('leaf', 'grid')), may hold values from -0.5 to 0.5
- expand_root: float32 [32768, 128], P(('leaf', 'grid')), may hold values from -0.5 to 0.5
- basis_root: float32 [32768, 256], P(('leaf', 'grid')), may hold values from -0.03125 to 0.03125
- pivot_root: float32 [32768], P(('leaf', 'grid')), may hold values from -2 to 2
- ranks_root: int32 [1, 2], replicated, may hold values from 32 to 128
Outputs:
- answer_leaf: float32 [8, 32768], P(None, ('leaf', 'grid'))
- answer_middle: float32 [8, 32768], P(None, ('leaf', 'grid'))
- answer_upper: float32 [8, 32768], P(None, ('leaf', 'grid'))
- answer_root: float32 [8, 32768], P(None, ('leaf', 'grid'))
Inputs may be any that keep to these rules, and one draw needn't show every extreme that they name: `targets_leaf`: within one leaf front the 1024 entries are distinct; each names a row of the parent front's row vector of 16384 rows. Split that vector's separator part and its update part each evenly, in order, over the parent's devices (leaf then grid); then the rows of one device name at most 4 rows held by any one of them, and exactly that many for some. `targets_middle`: within one middle front the entries are distinct; each names a row of the parent front's row vector of 32768 rows. Split likewise over the parent's devices, the rows of one device name at most 1 row held by any one of them, and exactly that many for some. `targets_upper`: within one upper front the entries are distinct; each names a row of the root separator. Split evenly in order over all devices, the rows of one device name at most 1 row held by any one of them, and exactly that many for some.
All inputs are finite; a program needn't handle non-finite values.
Results may differ from a plain program's by a relative error of at most 0.0003.
Values sent between devices are 32-bit elements; how exact they have to be, the bound alone decides.
A program may use at most 128 MiB of HBM per device.

v0:
```python
import functools

import jax
import jax.numpy as jnp
from jax import lax
from jax.experimental import pallas as pl
from jax.experimental.pallas import tpu as pltpu
from jax.sharding import PartitionSpec as P

MESH = pl.DeviceIdType.MESH
HIGHEST = lax.Precision.HIGHEST

NX, NZC, NY = 4, 16, 4

EXCHANGES = [
    ("x0", 4, 144),
    ("zp0", 4, 8),
    ("w0", 16, 8),
    ("a1", 16, 24),
    ("a2", 4, 80),
    ("b1", 16, 16),
    ("b2", 8, 32),
    ("c1", 16, 24),
    ("c2", 16, 32),
    ("cr_xc", 8, 48),
    ("cr_z", 8, 48),
    ("cr_m", 8, 16),
    ("cr_y", 4, 32),
    ("cr_g", 8, 48),
    ("f1_xc", 8, 16),
    ("f1_z", 8, 16),
    ("f1_y", 2, 8),
    ("f2_xc", 8, 24),
    ("f2_z", 8, 24),
    ("f2_y", 4, 24),
    ("f3_xc", 8, 24),
    ("f3_z", 8, 24),
    ("f3_y", 4, 24),
    ("d1", 16, 8),
    ("d2", 8, 16),
    ("e1", 16, 16),
    ("e2", 16, 16),
    ("u2_xc", 8, 16),
    ("u2_z", 8, 16),
    ("u2_y", 4, 16),
    ("g1", 16, 16),
    ("g2", 16, 16),
    ("u1_xc", 8, 16),
    ("u1_z", 8, 16),
    ("u1_y", 2, 16),
    ("h1", 8, 16),
    ("h2", 16, 8),
    ("u0_zc", 16, 8),
    ("u0_x", 4, 8),
]
NAMES = [entry[0] for entry in EXCHANGES]
SCATTERED = ["a1", "a2", "b1", "b2", "c1", "c2", "cr_xc", "d1", "d2", "e1", "e2", "g1", "g2", "h1", "h2", "u0_zc"]


def dot(a, b, ca, cb):
    return lax.dot_general(
        a, b, (((ca,), (cb,)), ((), ())), precision=HIGHEST, preferred_element_type=jnp.float32
    )


def mm(a, b):
    return dot(a, b, 1, 0)


def mm_t(a, b):
    return dot(a, b, 1, 1)


def t_mm(a, b):
    return dot(a, b, 0, 0)


def iota(shape, dim):
    return lax.broadcasted_iota(jnp.int32, shape, dim)


def ones_where(cond):
    return jnp.where(cond, 1.0, 0.0).astype(jnp.float32)


def stack16(v):
    return jnp.concatenate([v] * 16, axis=0)


def kernel(*refs):
    (
        src0, blk0, exp0, bas0, piv0, cpl0, rnk0, tgt0,
        src1, blk1, exp1, bas1, piv1, cpl1, rnk1, tgt1,
        src2, blk2, exp2, bas2, piv2, cpl2, rnk2, tgt2,
        src3, blk3, exp3, bas3, piv3, rnk3,
        out0, out1, out2, out3,
    ) = refs[:34]
    n_ex = len(EXCHANGES)
    recv = dict(zip(NAMES, refs[34 : 34 + n_ex]))
    send = dict(zip(SCATTERED, refs[34 + n_ex : 34 + n_ex + len(SCATTERED)]))
    send_sem, recv_sem = refs[34 + n_ex + len(SCATTERED) :]

    leaf = lax.axis_index("leaf")
    x = lax.axis_index("grid")
    y = leaf // 16
    zc = leaf % 16
    z = zc // 2
    c = zc % 2
    u = y // 2
    yb = y % 2
    xc = x * 2 + c
    k8 = yb * 4 + x
    k16 = y * 4 + x

    axes = {
        "x": (x, 4, lambda d: (leaf, d)),
        "zc": (zc, 16, lambda d: (y * 16 + d, x)),
        "xc": (xc, 8, lambda d: (leaf - c + d % 2, d // 2)),
        "z": (z, 8, lambda d: (y * 16 + d * 2 + c, x)),
        "y2": (yb, 2, lambda d: ((u * 2 + d) * 16 + zc, x)),
        "y4": (y, 4, lambda d: (d * 16 + zc, x)),
        "k8": (k8, 8, lambda d: ((u * 2 + d // 4) * 16 + zc, d % 4)),
        "k16": (k16, 16, lambda d: ((d // 4) * 16 + zc, d % 4)),
    }
    pending = []

    def copy_of(name, src, dst, dev):
        i = NAMES.index(name)
        return pltpu.make_async_remote_copy(
            src_ref=src,
            dst_ref=dst,
            send_sem=send_sem.at[i],
            recv_sem=recv_sem.at[i],
            device_id=dev,
            device_id_type=MESH,
        )

    def start(name, axis):
        me, n, dev = axes[axis]
        buf = recv[name]
        scattered = name in send

        def body(o, carry):
            d = lax.rem(me + o, n)
            src = send[name].at[d] if scattered else buf.at[me]
            copy_of(name, src, buf.at[me], dev(d)).start()
            return carry

        if scattered:
            buf[me] = send[name][me]
        lax.fori_loop(1, n, body, 0)
        pending.append((name, axis))

    def whole(name, axis):
        me, n, dev = axes[axis]
        part = recv[name].at[pl.ds(0, n - 1)]
        return copy_of(name, part, part, dev(lax.rem(me + 1, n)))

    def wait(name, axis):
        whole(name, axis).wait_recv()

    def share(name, axis, value):
        recv[name][axes[axis][0]] = value
        start(name, axis)

    def total(name, axis):
        wait(name, axis)
        return jnp.sum(recv[name][...], axis=0)

    barrier = pltpu.get_barrier_semaphore()

    def greet(axis):
        me, n, dev = axes[axis]

        def body(o, carry):
            pl.semaphore_signal(barrier, inc=1, device_id=dev(lax.rem(me + o, n)), device_id_type=MESH)
            return carry

        lax.fori_loop(1, n, body, 0)
        return n - 1

    greeted = greet("zc") + greet("k16") + greet("xc")

    lane = iota((1, 128), 1)

    def mask_of(ref, front, side):
        return ones_where(lane < ref[front, side])

    def column(row):
        n = row.shape[1]
        return jnp.transpose(jnp.broadcast_to(row, (128, n)))

    def packets(targets, sep_bits, kbits, ranked):
        piece = targets >> sep_bits
        within = targets & ((1 << sep_bits) - 1)
        label = piece * 128 + (within & 127) + 1
        owner = within >> 7
        if ranked:
            n = targets.shape[1]
            of = owner.astype(jnp.float32)
            same = column(of)[:, 0:1] == of
            before = iota((n, n), 0) < iota((n, n), 1)
            order = jnp.sum(ones_where(same & before), axis=0, keepdims=True)
            return of * 4.0 + order, label.astype(jnp.float32)
        sub = owner & 63
        pos = ((sub >> 2) << kbits) + ((owner >> 6) << 2) + (sub & 3)
        return pos.astype(jnp.float32), label.astype(jnp.float32)

    def place(pos, count):
        n = pos.shape[1]
        return ones_where(iota((count, n), 0).astype(jnp.float32) == pos)

    def label_rows(pos, label, kbits):
        n = pos.shape[1]
        ipos = pos.astype(jnp.int32)
        major = (ipos >> kbits).astype(jnp.float32)
        minor = (ipos & ((1 << kbits) - 1)).astype(jnp.float32)
        pick = ones_where(iota((16, n), 0).astype(jnp.float32) == major)
        spread = jnp.where(iota((n, 128), 1).astype(jnp.float32) == column(minor), column(label), 0.0)
        return mm(pick, spread)

    def fill_packets(name, pos, label, rows, kbits, couple):
        k = 1 << kbits
        at = place(pos, 16 * k)
        send[name][:, 0:k, :] = mm(at, couple).reshape(16, k, 128)
        lab = label_rows(pos, label, kbits)
        send[name][:, k : k + 8, :] = jnp.broadcast_to(lab[:, None, :], (16, 8, 128))
        return at

    pos0, lab0 = packets(tgt0[...], 13, 4, True)
    fill_packets("a1", pos0, lab0, 24, 4, cpl0[...])
    Q0, V0 = bas0[:, 0:128], bas0[:, 128:256]
    loc0 = mm(src0[...], blk0[...])
    x0_own = jnp.concatenate(
        [mm(src0[...], Q0), mm(loc0, V0), t_mm(exp0[...], V0)], axis=0
    )

    pl.semaphore_wait(barrier, greeted)
    share("x0", "x", x0_own)
    start("a1", "zc")

    V1 = bas1[:, 128:256]
    V2 = bas2[:, 128:256]
    cr1_own = t_mm(exp1[...], V1)
    cr2_own = t_mm(exp2[...], V2)
    P3 = exp3[...]
    scaled3 = P3 * column(piv3[...])
    m3_own = t_mm(P3, scaled3)
    send["cr_xc"][:, 0:16, :] = cr1_own.reshape(8, 16, 128)
    send["cr_xc"][:, 16:32, :] = cr2_own.reshape(8, 16, 128)
    send["cr_xc"][:, 32:48, :] = m3_own.reshape(8, 16, 128)
    start("cr_xc", "xc")

    mh0, mc0 = mask_of(rnk0, leaf, 0), mask_of(rnk0, leaf, 1)
    tot0 = total("x0", "x")
    hq0 = tot0[0:8] * mh0
    cr0 = tot0[16:144]
    w0 = (tot0[8:16] + mm(hq0, cr0)) * mc0
    share("w0", "zc", w0)
    z0 = (loc0 + mm_t(hq0, exp0[...])) * piv0[...]
    share("zp0", "x", mm(z0, exp0[...]))

    wait("a1", "zc")
    s_row = iota((256, 256), 0)
    r_col = iota((256, 256), 1)
    turn_a = ones_where(r_col == ((s_row >> 2) & 15) * 16 + (s_row >> 6) * 4 + (s_row & 3))
    moved = mm(turn_a, recv["a1"][:, 0:16, :].reshape(256, 128))
    labels = jnp.max(recv["a1"][:, 16:24, :], axis=1)
    send["a2"][:, 0:64, :] = moved.reshape(4, 64, 128)
    send["a2"][:, 64:80, :] = jnp.broadcast_to(labels[None], (4, 16, 128))
    start("a2", "x")

    cr_z_own = total("cr_xc", "xc")
    share("cr_z", "z", cr_z_own)

    pos1, lab1 = packets(tgt1[...], 14, 3, False)
    at1 = fill_packets("b1", pos1, lab1, 16, 3, cpl1[...])
    start("b1", "zc")
    pos2, lab2 = packets(tgt2[...], 15, 4, False)
    at2 = fill_packets("c1", pos2, lab2, 24, 4, cpl2[...])
    start("c1", "zc")

    wait("w0", "zc")
    wait("a2", "x")
    c0h = recv["a2"][:, 0:64, :].reshape(256, 128)
    lab_in = recv["a2"][:, 64:80, :].reshape(64, 128)
    spread = mm(ones_where(iota((256, 64), 1) == (iota((256, 64), 0) >> 2)), lab_in)
    mine = iota((256, 128), 1) == x * 4 + (iota((256, 128), 0) & 3)
    lab_col = jnp.sum(jnp.where(mine, spread, 0.0), axis=1, keepdims=True)
    oh0 = ones_where(iota((256, 256), 1).astype(jnp.float32) == lab_col - 1.0)
    front0 = (iota((128, 256), 0) >> 3) == ((iota((128, 256), 1) & 63) >> 2)
    e0 = jnp.where(front0, mm_t(recv["w0"][...].reshape(128, 128), c0h), 0.0)
    inc0 = -mm(jnp.sum(e0.reshape(16, 8, 256), axis=0), oh0)
    b1 = src1[...] + inc0[:, 0:128]
    upd1 = inc0[:, 128:256]
    loc1 = mm(b1, blk1[...])
    Q1 = bas1[:, 0:128]
    share("f1_xc", "xc", jnp.concatenate([mm(b1, Q1), mm(loc1, V1)], axis=0))
    send["d1"][...] = mm_t(at1, stack16(upd1)).reshape(16, 8, 128)
    start("d1", "zc")

    cr_sum = total("cr_z", "z")
    share("cr_m", "xc", cr_sum[0:16])
    share("cr_y", "y4", cr_sum[16:48])

    share("f1_z", "z", total("f1_xc", "xc"))

    wait("b1", "zc")
    turn_b = ones_where(iota((128, 128), 1) == (iota((128, 128), 0) & 15) * 8 + (iota((128, 128), 0) >> 4))
    send["b2"][:, 0:16, :] = mm(turn_b, recv["b1"][:, 0:8, :].reshape(128, 128)).reshape(8, 16, 128)
    send["b2"][:, 16:32, :] = jnp.broadcast_to(jnp.max(recv["b1"][:, 8:16, :], axis=1)[None], (8, 16, 128))
    start("b2", "k8")
    wait("d1", "zc")
    send["d2"][...] = mm(turn_b, recv["d1"][...].reshape(128, 128)).reshape(8, 16, 128)
    start("d2", "k8")
    wait("cr_y", "y4")
    cy = recv["cr_y"]
    share(
        "cr_g",
        "xc",
        jnp.concatenate(
            [
                cy[0, 0:16, :] + cy[1, 0:16, :],
                cy[2, 0:16, :] + cy[3, 0:16, :],
                (cy[0, 16:32, :] + cy[1, 16:32, :]) + (cy[2, 16:32, :] + cy[3, 16:32, :]),
            ],
            axis=0,
        ),
    )
    wait("c1", "zc")
    turn_c = ones_where(r_col == (s_row & 15) * 16 + (s_row >> 4))
    send["c2"][:, 0:16, :] = mm(turn_c, recv["c1"][:, 0:16, :].reshape(256, 128)).reshape(16, 16, 128)
    send["c2"][:, 16:32, :] = jnp.broadcast_to(jnp.max(recv["c1"][:, 16:24, :], axis=1)[None], (16, 16, 128))
    start("c2", "k16")

    wait("cr_m", "xc")
    cr1 = recv["cr_m"][...].reshape(128, 128)
    mh1, mc1 = mask_of(rnk1, y, 0), mask_of(rnk1, y, 1)
    tot1 = total("f1_z", "z")
    hq1 = tot1[0:8] * mh1
    share("f1_y", "y2", (tot1[8:16] + mm(hq1, cr1)) * mc1)
    z1 = (loc1 + mm_t(hq1, exp1[...])) * piv1[...]
    zp1_own = mm(z1, exp1[...])

    wait("b2", "k8")
    c1h = recv["b2"][:, 0:16, :].reshape(128, 128)
    lab_in = recv["b2"][:, 16:32, :].reshape(128, 128)
    lab_col = jnp.sum(jnp.where(iota((128, 128), 1) == k8, lab_in, 0.0), axis=1, keepdims=True)
    oh1 = ones_where(iota((128, 256), 1).astype(jnp.float32) == lab_col - 1.0)
    front1 = (iota((16, 128), 0) >> 3) == (iota((16, 128), 1) >> 6)
    wait("d2", "k8")
    came1 = jnp.transpose(recv["d2"][...].reshape(128, 128))[0:8]
    wait("f1_y", "y2")
    e1 = jnp.where(front1, mm_t(recv["f1_y"][...].reshape(16, 128), c1h), 0.0)
    inc1 = mm(came1 - (e1[0:8] + e1[8:16]), oh1)
    b2 = src2[...] + inc1[:, 0:128]
    upd2 = inc1[:, 128:256]
    loc2 = mm(b2, blk2[...])
    Q2 = bas2[:, 0:128]
    share("f2_xc", "xc", jnp.concatenate([mm(b2, Q2), mm(loc2, V2), zp1_own], axis=0))
    send["e1"][...] = mm_t(at2, stack16(upd2)).reshape(16, 16, 128)
    start("e1", "zc")
    share("f2_z", "z", total("f2_xc", "xc"))
    wait("e1", "zc")
    send["e2"][...] = mm(turn_c, recv["e1"][...].reshape(256, 128)).reshape(16, 16, 128)
    start("e2", "k16")
    wait("cr_g", "xc")
    cg = recv["cr_g"]
    cr2_each = [cg[:, 0:16, :].reshape(128, 128), cg[:, 16:32, :].reshape(128, 128)]
    m3 = cg[:, 32:48, :].reshape(128, 128)
    wait("c2", "k16")
    c2h = recv["c2"][:, 0:16, :].reshape(256, 128)
    lab_in = recv["c2"][:, 16:32, :].reshape(256, 128)
    lab_col = jnp.sum(jnp.where(iota((256, 128), 1) == k16, lab_in, 0.0), axis=1, keepdims=True)
    oh2 = ones_where(iota((256, 128), 1).astype(jnp.float32) == lab_col - 1.0)
    front2 = (iota((16, 256), 0) >> 3) == (iota((16, 256), 1) >> 7)
    share("f2_y", "y4", total("f2_z", "z"))
    wait("f2_y", "y4")
    fy = recv["f2_y"]
    hq2_each, w2_each = [], []
    for v in range(2):
        t1 = fy[2 * v, 0:8, :] + fy[2 * v + 1, 0:8, :]
        t2 = fy[2 * v, 8:16, :] + fy[2 * v + 1, 8:16, :]
        hq = t1 * mask_of(rnk2, v, 0)
        hq2_each.append(hq)
        w2_each.append((t2 + mm(hq, cr2_each[v])) * mask_of(rnk2, v, 1))
    zp1 = fy[y, 16:24, :]
    first = u == 0
    hq2 = jnp.where(first, hq2_each[0], hq2_each[1])
    cr2 = jnp.where(first, cr2_each[0], cr2_each[1])
    mh2, mc2 = mask_of(rnk2, u, 0), mask_of(rnk2, u, 1)
    z2 = (loc2 + mm_t(hq2, exp2[...])) * piv2[...]
    zp2_own = mm(z2, exp2[...])

    e2 = jnp.where(front2, mm_t(jnp.concatenate(w2_each, axis=0), c2h), 0.0)
    wait("e2", "k16")
    came2 = jnp.transpose(recv["e2"][...].reshape(256, 128))[0:8]
    b3 = src3[...] + mm(came2 - (e2[0:8] + e2[8:16]), oh2)
    loc3 = mm(b3, blk3[...])
    Q3 = bas3[:, 0:128]
    share("f3_xc", "xc", jnp.concatenate([mm(b3, Q3), mm(loc3 * piv3[...], P3), zp2_own], axis=0))
    share("f3_z", "z", total("f3_xc", "xc"))
    share("f3_y", "y4", total("f3_z", "z"))
    wait("f3_y", "y4")
    fy = recv["f3_y"]
    lower = fy[0] + fy[1]
    upper = fy[2] + fy[3]
    mh3 = mask_of(rnk3, 0, 0)
    both = lower + upper
    hq3 = both[0:8] * mh3
    zp2 = jnp.where(first, lower[16:24], upper[16:24])
    g3 = (both[8:16] + mm(hq3, m3)) * mh3
    z3 = (loc3 + mm_t(hq3, P3)) * piv3[...]
    x3 = mm_t(z3, blk3[...]) + mm_t(g3, Q3)
    out3[...] = x3

    vals = mm_t(x3, oh2)
    share("u2_xc", "xc", mm(jnp.where(front2, jnp.concatenate([vals, vals], axis=0), 0.0), c2h))
    send["g1"][...] = mm_t(oh2, stack16(x3)).reshape(16, 16, 128)
    start("g1", "k16")
    share("u2_z", "z", total("u2_xc", "xc"))
    wait("g1", "k16")
    send["g2"][...] = mm(turn_c, recv["g1"][...].reshape(256, 128)).reshape(16, 16, 128)
    start("g2", "zc")
    share("u2_y", "y4", total("u2_z", "z"))
    s2_all = total("u2_y", "y4")
    s2 = jnp.where(first, s2_all[0:8], s2_all[8:16]) * mc2
    g2 = (zp2 - mm_t(s2, cr2)) * mh2
    r2 = z2 - mm_t(s2, V2)
    x2 = mm_t(r2, blk2[...]) + mm_t(g2, Q2)
    out2[...] = x2
    wait("g2", "zc")
    xu2 = t_mm(recv["g2"][...].reshape(256, 128), at2)[0:8]

    full2 = jnp.concatenate([x2, xu2], axis=1)
    vals = mm_t(full2, oh1)
    share("u1_xc", "xc", mm(jnp.where(front1, jnp.concatenate([vals, vals], axis=0), 0.0), c1h))
    send["h1"][...] = mm_t(oh1, stack16(full2)).reshape(8, 16, 128)
    start("h1", "k8")
    share("u1_z", "z", total("u1_xc", "xc"))
    wait("h1", "k8")
    send["h2"][...] = t_mm(turn_b, recv["h1"][...].reshape(128, 128)).reshape(16, 8, 128)
    start("h2", "zc")
    share("u1_y", "y2", total("u1_z", "z"))
    s1_all = total("u1_y", "y2")
    s1 = jnp.where(yb == 0, s1_all[0:8], s1_all[8:16]) * mc1
    g1 = (zp1 - mm_t(s1, cr1)) * mh1
    r1 = z1 - mm_t(s1, V1)
    x1 = mm_t(r1, blk1[...]) + mm_t(g1, Q1)
    out1[...] = x1
    wait("h2", "zc")
    xu1 = t_mm(recv["h2"][...].reshape(128, 128), at1)[0:8]

    vals = mm_t(jnp.concatenate([x1, xu1], axis=1), oh0)
    send["u0_zc"][...] = mm(jnp.where(front0, stack16(vals), 0.0), c0h).reshape(16, 8, 128)
    start("u0_zc", "zc")
    zp0 = total("zp0", "x")
    share("u0_x", "x", total("u0_zc", "zc"))
    s0 = total("u0_x", "x") * mc0
    g0 = (zp0 - mm_t(s0, cr0)) * mh0
    r0 = z0 - mm_t(s0, V0)
    out0[...] = mm_t(r0, blk0[...]) + mm_t(g0, Q0)

    for name, axis in pending:
        whole(name, axis).wait_send()


def shards(*args):
    args = list(args)
    for i in (4, 12, 20, 28):
        args[i] = args[i].reshape(1, -1)
    for i in (7, 15, 23):
        args[i] = args[i].reshape(1, -1)
    ranks = (6, 14, 22, 29)
    vmem = pl.BlockSpec(memory_space=pltpu.VMEM)
    smem = pl.BlockSpec(memory_space=pltpu.SMEM)
    sizes = {name: (n, rows, 128) for name, n, rows in EXCHANGES}
    scratch = [pltpu.VMEM(sizes[name], jnp.float32) for name in NAMES]
    scratch += [pltpu.VMEM(sizes[name], jnp.float32) for name in SCATTERED]
    scratch += [pltpu.SemaphoreType.DMA((len(NAMES),)), pltpu.SemaphoreType.DMA((len(NAMES),))]
    return tuple(
        pl.pallas_call(
            kernel,
            out_shape=[jax.ShapeDtypeStruct((8, 128), jnp.float32)] * 4,
            in_specs=[smem if i in ranks else vmem for i in range(len(args))],
            out_specs=[vmem] * 4,
            scratch_shapes=scratch,
            compiler_params=pltpu.CompilerParams(
                collective_id=0, has_side_effects=True, vmem_limit_bytes=48 * 1024 * 1024
            ),
            name="solve",
        )(*args)
    )


def solution(mesh):
    columns = P(None, ("leaf", "grid"))
    rows = P(("leaf", "grid"), None)
    flat = P(("leaf", "grid"))
    level = (columns, rows, rows, rows, flat, rows, P(), flat)
    in_specs = level * 3 + (columns, rows, rows, rows, flat, P())
    return jax.shard_map(
        shards, mesh=mesh, in_specs=in_specs, out_specs=(columns,) * 4, check_vma=False
    )
```

profile of v0, /device:TPU:1, one launch (start us, length us, event | category | flops | bytes accessed | tf_op | source)
XLA Modules:
  0.0 126.8 jit_solution(5890907588114392147)
XLA Ops:
  0.6 0.7 copy-done.28
  1.3 0.1 copy.35.refs_14_
  1.4 0.6 copy-done.29
  2.1 0.1 copy.34.refs_6_
  2.2 0.5 copy-done.15
  2.7 0.0 copy-done.16
  2.7 0.0 copy-done.17
  2.7 0.0 copy-done.18
  2.7 0.0 copy-done.20
  2.8 0.0 copy-done.23
  2.8 0.0 copy-done.25
  2.8 0.0 copy-done.27
  2.8 0.9 copy-done
  3.7 0.9 copy-done.1
  4.6 0.9 copy-done.2
  5.6 0.9 copy-done.3
  6.5 0.9 copy-done.4
  7.4 0.8 copy-done.5
  8.2 0.8 copy-done.6
  9.0 0.8 copy-done.7
  9.9 0.8 copy-done.8
  10.7 0.8 copy-done.9
  11.6 0.8 copy-done.10
  12.4 0.8 copy-done.11
  13.2 0.8 copy-done.12
  14.1 0.8 copy-done.13
  14.9 0.8 copy-done.14
  15.8 108.6 %solve.1 = (f32[8,128]{1,0:T(8,128)S(1)}, f32[8,128]{1,0:T(8,128)S(1)}, f32[8,128]{1,0:T(8,128)S(1)}, f32[8,128]{1,0:T(8,128)S(1)}) custom-call(f32[8,128]{1,0:T(8,128)S(1)} %copy-done.15, f32[128,128]{1,0:T(8,128)S(1)} %copy-done.5, f32[128,128]{1,0:T(8,128)S(1)} %copy-done.6, f32[128,256]{1,0:T(8,128)S(1)} %copy-done, f32[1,128]{1,0:T(1,128)S(1)} %bitcast.8, ...), custom_call_target="tpu_custom_call" | custom-call | tf_op jit(solution)/shard_map/solve/pallas_call | solution.py:482
  124.4 0.6 copy.40
  125.0 0.6 copy.41
  125.6 0.6 copy.42
  126.2 0.6 copy.43
  (35 shorter events, 0.1 us)
Async XLA Ops:
  0.6 0.7 copy-start.28
  1.3 0.7 copy-start.29
  2.0 0.7 copy-start.15
  2.0 0.7 copy-start.16
  2.0 0.7 copy-start.17
  2.0 0.7 copy-start.18
  2.0 0.7 copy-start.19
  2.0 0.7 copy-start.20
  2.0 0.7 copy-start.21
  2.0 0.7 copy-start.22
  2.0 0.7 copy-start.23
  2.1 0.7 copy-start.24
  2.1 0.7 copy-start.25
  2.1 0.7 copy-start.26
  2.1 0.7 copy-start.27
  2.8 0.9 copy-start
  3.7 0.9 copy-start.1
  4.6 0.9 copy-start.2
  5.6 0.9 copy-start.3
  6.5 0.9 copy-start.4
  7.4 0.8 copy-start.5
  8.2 0.8 copy-start.6
  9.0 0.8 copy-start.7
  9.9 0.8 copy-start.8
  10.7 0.8 copy-start.9
  11.6 0.8 copy-start.10
  12.4 0.8 copy-start.11
  13.2 0.8 copy-start.12
  14.1 0.8 copy-start.13
  14.9 0.8 copy-start.14
where the time goes:
time: 128 us; the launch traced here: 127 us
  Pallas kernels  109 us (85%)
  local copies, waits for them, and re-layouts  17.4 us (14%)
    pallas_call x1, Pallas kernels, shards(): pl.pallas_call(kernel, out_shape=[jax.ShapeDtypeStruct((8, 128), jnp.floa...  109 us
    unnamed x66, local copies, waits for them, and re-layouts  17.4 us

commit v1 on v0

--- a/solution.py
+++ b/solution.py
@@ -87,18 +87,46 @@
     return jnp.concatenate([v] * 16, axis=0)
 
 
+class Operand:
+    def __init__(self, i, *refs):
+        self.vmem = refs[31 + i]
+        self.copy = pltpu.make_async_copy(refs[i], self.vmem, refs[-1].at[i])
+        self.start = self.copy.start
+        self.here = False
+
+    def ready(self):
+        if not self.here:
+            self.copy.wait()
+            self.here = True
+
+    def __getitem__(self, index):
+        self.ready()
+        return self.vmem[index]
+
+    def rank(self, side, front):
+        if self.vmem.shape[1] == 2 and self.vmem.shape[0] < 3:
+            column = self[:, side : side + 1].astype(jnp.float32)
+            return jnp.sum(jnp.where(iota(column.shape, 0) == front, column, 0.0), axis=0, keepdims=True)
+        row = self[side : side + 1, :].astype(jnp.float32)
+        return jnp.sum(jnp.where(iota(row.shape, 1) == front, row, 0.0), axis=1, keepdims=True)
+
+
 def kernel(*refs):
     (
         src0, blk0, exp0, bas0, piv0, cpl0, rnk0, tgt0,
         src1, blk1, exp1, bas1, piv1, cpl1, rnk1, tgt1,
         src2, blk2, exp2, bas2, piv2, cpl2, rnk2, tgt2,
         src3, blk3, exp3, bas3, piv3, rnk3,
-        out0, out1, out2, out3,
-    ) = refs[:34]
+        out,
+    ) = [Operand(i, *refs) for i in range(30)] + list(refs[30:31])
+    refs = refs[61:]
     n_ex = len(EXCHANGES)
-    recv = dict(zip(NAMES, refs[34 : 34 + n_ex]))
-    send = dict(zip(SCATTERED, refs[34 + n_ex : 34 + n_ex + len(SCATTERED)]))
-    send_sem, recv_sem = refs[34 + n_ex + len(SCATTERED) :]
+    recv = dict(zip(NAMES, refs[:n_ex]))
+    send = dict(zip(SCATTERED, refs[n_ex : n_ex + len(SCATTERED)]))
+    send_sem, recv_sem = refs[n_ex + len(SCATTERED) : n_ex + len(SCATTERED) + 2]
+
+    for operand in (tgt0, cpl0, src0, blk0, bas0, exp0):
+        operand.start()
 
     leaf = lax.axis_index("leaf")
     x = lax.axis_index("grid")
@@ -181,10 +209,16 @@
 
     greeted = greet("zc") + greet("k16") + greet("xc")
 
+    for operand in (
+        exp1, bas1, exp2, bas2, exp3, piv3, rnk0, piv0, tgt1, cpl1, tgt2, cpl2, src1, blk1, rnk1, piv1,
+        src2, blk2, rnk2, piv2, src3, blk3, bas3, rnk3,
+    ):
+        operand.start()
+
     lane = iota((1, 128), 1)
 
     def mask_of(ref, front, side):
-        return ones_where(lane < ref[front, side])
+        return ones_where(lane.astype(jnp.float32) < ref.rank(side, front))
 
     def column(row):
         n = row.shape[1]
@@ -412,7 +446,7 @@
     g3 = (both[8:16] + mm(hq3, m3)) * mh3
     z3 = (loc3 + mm_t(hq3, P3)) * piv3[...]
     x3 = mm_t(z3, blk3[...]) + mm_t(g3, Q3)
-    out3[...] = x3
+    out[3] = x3
 
     vals = mm_t(x3, oh2)
     share("u2_xc", "xc", mm(jnp.where(front2, jnp.concatenate([vals, vals], axis=0), 0.0), c2h))
@@ -428,7 +462,7 @@
     g2 = (zp2 - mm_t(s2, cr2)) * mh2
     r2 = z2 - mm_t(s2, V2)
     x2 = mm_t(r2, blk2[...]) + mm_t(g2, Q2)
-    out2[...] = x2
+    out[2] = x2
     wait("g2", "zc")
     xu2 = t_mm(recv["g2"][...].reshape(256, 128), at2)[0:8]
 
@@ -447,7 +481,7 @@
     g1 = (zp1 - mm_t(s1, cr1)) * mh1
     r1 = z1 - mm_t(s1, V1)
     x1 = mm_t(r1, blk1[...]) + mm_t(g1, Q1)
-    out1[...] = x1
+    out[1] = x1
     wait("h2", "zc")
     xu1 = t_mm(recv["h2"][...].reshape(128, 128), at1)[0:8]
 
@@ -459,10 +493,18 @@
     s0 = total("u0_x", "x") * mc0
     g0 = (zp0 - mm_t(s0, cr0)) * mh0
     r0 = z0 - mm_t(s0, V0)
-    out0[...] = mm_t(r0, blk0[...]) + mm_t(g0, Q0)
+    out[0] = mm_t(r0, blk0[...]) + mm_t(g0, Q0)
 
     for name, axis in pending:
         whole(name, axis).wait_send()
+
+
+def apart(answers, *refs):
+    copies = [pltpu.make_async_copy(answers.at[k], refs[k], refs[4].at[k]) for k in range(4)]
+    for copy in copies:
+        copy.start()
+    for copy in copies:
+        copy.wait()
 
 
 def shards(*args):
@@ -471,25 +513,36 @@
         args[i] = args[i].reshape(1, -1)
     for i in (7, 15, 23):
         args[i] = args[i].reshape(1, -1)
-    ranks = (6, 14, 22, 29)
+    for i in (6, 14):
+        args[i] = args[i].T
+    hbm = pl.BlockSpec(memory_space=pltpu.HBM)
     vmem = pl.BlockSpec(memory_space=pltpu.VMEM)
-    smem = pl.BlockSpec(memory_space=pltpu.SMEM)
     sizes = {name: (n, rows, 128) for name, n, rows in EXCHANGES}
-    scratch = [pltpu.VMEM(sizes[name], jnp.float32) for name in NAMES]
+    scratch = [pltpu.VMEM(arg.shape, arg.dtype) for arg in args]
+    scratch += [pltpu.VMEM(sizes[name], jnp.float32) for name in NAMES]
     scratch += [pltpu.VMEM(sizes[name], jnp.float32) for name in SCATTERED]
     scratch += [pltpu.SemaphoreType.DMA((len(NAMES),)), pltpu.SemaphoreType.DMA((len(NAMES),))]
+    scratch += [pltpu.SemaphoreType.DMA((len(args),))]
+    answers = pl.pallas_call(
+        kernel,
+        out_shape=jax.ShapeDtypeStruct((4, 8, 128), jnp.float32),
+        in_specs=[hbm] * len(args),
+        out_specs=vmem,
+        scratch_shapes=scratch,
+        compiler_params=pltpu.CompilerParams(
+            collective_id=0, has_side_effects=True, vmem_limit_bytes=67043328
+        ),
+        name="solve",
+    )(*args)
     return tuple(
         pl.pallas_call(
-            kernel,
+            apart,
             out_shape=[jax.ShapeDtypeStruct((8, 128), jnp.float32)] * 4,
-            in_specs=[smem if i in ranks else vmem for i in range(len(args))],
-            out_specs=[vmem] * 4,
-            scratch_shapes=scratch,
-            compiler_params=pltpu.CompilerParams(
-                collective_id=0, has_side_effects=True, vmem_limit_bytes=48 * 1024 * 1024
-            ),
-            name="solve",
-        )(*args)
+            in_specs=[vmem],
+            out_specs=[hbm] * 4,
+            scratch_shapes=[pltpu.SemaphoreType.DMA((4,))],
+            name="apart",
+        )(answers)
     )
 
 

time: 128 us -> 111 us (0.87)
  local copies, waits for them, and re-layouts: 17.4 us -> 0 us
    unnamed x66 -> x0, local copies, waits for them, and re-layouts: 17.4 us -> none
    pallas_call x1 -> x2, Pallas kernels: 109 us -> 110 us  [the longest x1 109 us: shards(): pl.pallas_call(kernel, out_shape=jax.ShapeDtypeStruct((4, 8, 128), jnp.fl...]
where the time goes in v1:
time: 111 us
  Pallas kernels  110 us (99%)
    pallas_call x1, Pallas kernels, shards(): pl.pallas_call(kernel, out_shape=jax.ShapeDtypeStruct((4, 8, 128), jnp.fl...  109 us

profile of v1, /device:TPU:1, one launch (start us, length us, event | category | flops | bytes accessed | tf_op | source)
XLA Modules:
  0.0 110.7 jit_solution(16991244860016303627)
XLA Ops:
  0.6 108.7 %solve.1.answers = f32[4,8,128]{2,1,0:T(8,128)} custom-call(f32[8,128]{1,0:T(8,128)} %refs_0_.1, f32[128,128]{1,0:T(8,128)} %refs_1_.1, f32[128,128]{1,0:T(8,128)} %refs_2_.1, f32[128,256]{1,0:T(8,128)} %refs_3_.1, f32[1,128]{1,0:T(1,128)} %bitcast.12, f32[256,128]{1,0:T(8,128)} %refs_5_.1, s32[2,64]{1,0:T(2,128)} %bitcast.9, s32[1,256]{1,0:T(1,128)} %bitcast.10, ...), custom_call_target="tpu_custom_call" | custom-call | tf_op jit(solution)/shard_map/solve/pallas_call | solution.py:526
  109.4 1.4 %apart.1 = (f32[8,128]{1,0:T(8,128)}, f32[8,128]{1,0:T(8,128)}, f32[8,128]{1,0:T(8,128)}, f32[8,128]{1,0:T(8,128)}) custom-call(f32[4,8,128]{2,1,0:T(8,128)} %solve.1.answers), custom_call_target="tpu_custom_call" | custom-call | tf_op jit(solution)/shard_map/apart/pallas_call | solution.py:538

commit v2 on v1

v2 whole, which is shorter than its diff:
```python
import functools

import jax
import jax.numpy as jnp
from jax import lax
from jax.experimental import pallas as pl
from jax.experimental.pallas import tpu as pltpu
from jax.sharding import PartitionSpec as P

MESH = pl.DeviceIdType.MESH
HIGHEST = lax.Precision.HIGHEST

NX, NZC, NY = 4, 16, 4

EXCHANGES = [
    ("x0a", 4, 8, 8),
    ("x0b", 4, 8, 8),
    ("x0c", 4, 128, 128),
    ("zp0", 4, 8, 8),
    ("w0", 16, 8, 8),
    ("a1", 16, 24, 17),
    ("a2", 4, 80, 80),
    ("b1", 16, 16, 9),
    ("b2", 8, 32, 32),
    ("c1", 16, 24, 17),
    ("c2", 16, 32, 32),
    ("q_xc", 8, 16, 16),
    ("q_z", 8, 16, 16),
    ("q_g", 8, 16, 16),
    ("r_xc", 8, 32, 32),
    ("r_z", 8, 32, 32),
    ("r_y", 4, 32, 32),
    ("r_g", 8, 48, 48),
    ("f1_xc", 8, 16, 16),
    ("f1_z", 8, 16, 16),
    ("f1_y", 2, 8, 8),
    ("f2_xc", 8, 24, 24),
    ("f2_z", 8, 24, 24),
    ("f2_y", 4, 24, 24),
    ("f3_xc", 8, 24, 24),
    ("f3_z", 8, 24, 24),
    ("f3_y", 4, 24, 24),
    ("d1", 16, 1, 1),
    ("d2", 8, 1, 1),
    ("e1", 16, 1, 1),
    ("e2", 16, 1, 1),
    ("u2_xc", 8, 16, 16),
    ("u2_z", 8, 16, 16),
    ("u2_y", 4, 16, 16),
    ("g1", 16, 1, 1),
    ("g2", 16, 1, 1),
    ("u1_xc", 8, 16, 16),
    ("u1_z", 8, 16, 16),
    ("u1_y", 2, 16, 16),
    ("h1", 8, 1, 1),
    ("h2", 16, 1, 1),
    ("u0_zc", 16, 8, 8),
    ("u0_x", 4, 8, 8),
]
NAMES = [entry[0] for entry in EXCHANGES]
SENT = {entry[0]: entry[3] for entry in EXCHANGES}
SCATTERED = [
    "a1", "a2", "b1", "b2", "c1", "c2", "q_xc", "r_xc", "d1", "d2", "e1", "e2", "g1", "g2", "h1", "h2", "u0_zc"
]


def dot(a, b, ca, cb):
    return lax.dot_general(
        a, b, (((ca,), (cb,)), ((), ())), precision=HIGHEST, preferred_element_type=jnp.float32
    )


def mm(a, b):
    return dot(a, b, 1, 0)


def mm_t(a, b):
    return dot(a, b, 1, 1)


def t_mm(a, b):
    return dot(a, b, 0, 0)


def iota(shape, dim):
    return lax.broadcasted_iota(jnp.int32, shape, dim)


def ones_where(cond):
    return jnp.where(cond, 1.0, 0.0).astype(jnp.float32)


def stack16(v):
    return jnp.concatenate([v] * 16, axis=0)


class Operand:
    def __init__(self, i, *refs):
        self.vmem = refs[31 + i]
        self.copy = pltpu.make_async_copy(refs[i], self.vmem, refs[-1].at[i])
        self.start = self.copy.start
        self.here = False

    def ready(self):
        if not self.here:
            self.copy.wait()
            self.here = True

    def __getitem__(self, index):
        self.ready()
        return self.vmem[index]

    def rank(self, side, front):
        if self.vmem.shape[1] == 2 and self.vmem.shape[0] < 3:
            column = self[:, side : side + 1].astype(jnp.float32)
            return jnp.sum(jnp.where(iota(column.shape, 0) == front, column, 0.0), axis=0, keepdims=True)
        row = self[side : side + 1, :].astype(jnp.float32)
        return jnp.sum(jnp.where(iota(row.shape, 1) == front, row, 0.0), axis=1, keepdims=True)


def kernel(*refs):
    (
        src0, blk0, exp0, bas0, piv0, cpl0, rnk0, tgt0,
        src1, blk1, exp1, bas1, piv1, cpl1, rnk1, tgt1,
        src2, blk2, exp2, bas2, piv2, cpl2, rnk2, tgt2,
        src3, blk3, exp3, bas3, piv3, rnk3,
        out,
    ) = [Operand(i, *refs) for i in range(30)] + list(refs[30:31])
    refs = refs[61:]
    n_ex = len(EXCHANGES)
    recv = dict(zip(NAMES, refs[:n_ex]))
    send = dict(zip(SCATTERED, refs[n_ex : n_ex + len(SCATTERED)]))
    send_sem, recv_sem = refs[n_ex + len(SCATTERED) : n_ex + len(SCATTERED) + 2]

    for operand in (tgt0, cpl0, src0, blk0, bas0, exp0):
        operand.start()

    leaf = lax.axis_index("leaf")
    x = lax.axis_index("grid")
    y = leaf // 16
    zc = leaf % 16
    z = zc // 2
    c = zc % 2
    u = y // 2
    yb = y % 2
    xc = x * 2 + c
    k8 = yb * 4 + x
    k16 = y * 4 + x

    axes = {
        "x": (x, 4, lambda d: (leaf, d)),
        "zc": (zc, 16, lambda d: (y * 16 + d, x)),
        "xc": (xc, 8, lambda d: (leaf - c + d % 2, d // 2)),
        "z": (z, 8, lambda d: (y * 16 + d * 2 + c, x)),
        "y2": (yb, 2, lambda d: ((u * 2 + d) * 16 + zc, x)),
        "y4": (y, 4, lambda d: (d * 16 + zc, x)),
        "k8": (k8, 8, lambda d: ((u * 2 + d // 4) * 16 + zc, d % 4)),
        "k16": (k16, 16, lambda d: ((d // 4) * 16 + zc, d % 4)),
    }
    pending = []

    def copy_of(name, src, dst, dev):
        i = NAMES.index(name)
        return pltpu.make_async_remote_copy(
            src_ref=src,
            dst_ref=dst,
            send_sem=send_sem.at[i],
            recv_sem=recv_sem.at[i],
            device_id=dev,
            device_id_type=MESH,
        )

    def start(name, axis):
        me, n, dev = axes[axis]
        buf = recv[name]
        scattered = name in send

        def body(o, carry):
            d = lax.rem(me + o, n)
            rows = pl.ds(0, SENT[name])
            src = send[name].at[d, rows] if scattered else buf.at[me, rows]
            copy_of(name, src, buf.at[me, rows], dev(d)).start()
            return carry

        if scattered:
            buf[me] = send[name][me]
        lax.fori_loop(1, n, body, 0)
        pending.append((name, axis))

    def whole(name, axis):
        me, n, dev = axes[axis]
        part = recv[name].at[pl.ds(0, n - 1), pl.ds(0, SENT[name])]
        return copy_of(name, part, part, dev(lax.rem(me + 1, n)))

    def wait(name, axis):
        whole(name, axis).wait_recv()

    def share(name, axis, value):
        recv[name][axes[axis][0]] = value
        start(name, axis)

    def total(name, axis):
        wait(name, axis)
        return jnp.sum(recv[name][...], axis=0)

    barrier = pltpu.get_barrier_semaphore()

    def greet(axis):
        me, n, dev = axes[axis]

        def body(o, carry):
            pl.semaphore_signal(barrier, inc=1, device_id=dev(lax.rem(me + o, n)), device_id_type=MESH)
            return carry

        lax.fori_loop(1, n, body, 0)
        return n - 1

    greeted = greet("zc") + greet("k16") + greet("xc")

    for operand in (
        exp1, bas1, exp2, bas2, exp3, piv3, rnk0, piv0, tgt1, cpl1, tgt2, cpl2, src1, blk1, rnk1, piv1,
        src2, blk2, rnk2, piv2, src3, blk3, bas3, rnk3,
    ):
        operand.start()

    lane = iota((1, 128), 1)

    def mask_of(ref, front, side):
        return ones_where(lane.astype(jnp.float32) < ref.rank(side, front))

    def column(row):
        n = row.shape[1]
        return jnp.transpose(jnp.broadcast_to(row, (128, n)))

    def packets(targets, sep_bits, kbits, ranked):
        piece = targets >> sep_bits
        within = targets & ((1 << sep_bits) - 1)
        label = piece * 128 + (within & 127) + 1
        owner = within >> 7
        if ranked:
            n = targets.shape[1]
            of = owner.astype(jnp.float32)
            same = column(of)[:, 0:1] == of
            before = iota((n, n), 0) < iota((n, n), 1)
            order = jnp.sum(ones_where(same & before), axis=0, keepdims=True)
            return of * 4.0 + order, label.astype(jnp.float32)
        sub = owner & 63
        pos = ((sub >> 2) << kbits) + ((owner >> 6) << 2) + (sub & 3)
        return pos.astype(jnp.float32), label.astype(jnp.float32)

    def place(pos, count):
        n = pos.shape[1]
        return ones_where(iota((count, n), 0).astype(jnp.float32) == pos)

    def halves(pos, kbits):
        ipos = pos.astype(jnp.int32)
        return (ipos >> kbits).astype(jnp.float32), (ipos & ((1 << kbits) - 1)).astype(jnp.float32)

    def fill_packets(name, pos, label, kbits, couple):
        k = 1 << kbits
        n = pos.shape[1]
        send[name][:, 0:k, :] = mm(place(pos, 16 * k), couple).reshape(16, k, 128)
        major, minor = halves(pos, kbits)
        pick = ones_where(iota((16, n), 0).astype(jnp.float32) == major)
        minor_col = column(minor)
        spread = jnp.where(iota((n, 128), 1).astype(jnp.float32) == minor_col, column(label), 0.0)
        labels = mm(pick, spread)
        send[name][:, k : k + 8, :] = jnp.broadcast_to(labels[:, None, :], (16, 8, 128))
        return pick, (iota((n, 128), 1) >> 3).astype(jnp.float32) == minor_col

    def chain(qv, w, p):
        return jnp.concatenate([qv, mm(w, p)], axis=1)

    fold = ones_where((iota((128, 128), 0) & 7) == (iota((128, 128), 1) & 7))

    def blocks_are(shape_rows, of_row):
        return (iota((shape_rows, 128), 1) >> 3) == of_row(iota((shape_rows, 128), 0))

    def values_up(name, update, pick, block):
        rows = jnp.where(block, jnp.transpose(stack16(update)), 0.0)
        send[name][...] = mm(pick, rows).reshape(16, 1, 128)
        start(name, "zc")

    def values_on(name, got, outer, inner, axis):
        bits = inner.bit_length() - 1
        rows = jnp.concatenate([recv[got][...].reshape(inner, 128)] * outer, axis=0)
        rows = jnp.where(blocks_are(outer * inner, lambda r: r >> bits), rows, 0.0)
        rows = jnp.where(blocks_are(outer * inner, lambda r: r & (inner - 1)), mm(rows, fold), 0.0)
        send[name][...] = jnp.sum(rows.reshape(outer, inner, 128), axis=1).reshape(outer, 1, 128)
        start(name, axis)

    def values_in(got, k):
        rows = jnp.broadcast_to(recv[got][...], (k, 16, 128)).reshape(k * 16, 128)
        rows = jnp.where(blocks_are(k * 16, lambda r: r & 15), rows, 0.0)
        return mm_t(fold[0:8], rows)

    def values_down(name, onehot, full, k, axis):
        rows = mm_t(onehot, stack16(full))
        rows = jnp.where(blocks_are(k * 16, lambda r: r & 15), rows, 0.0)
        send[name][...] = jnp.sum(rows.reshape(k, 16, 128), axis=1).reshape(k, 1, 128)
        start(name, axis)

    def values_back(got, pick, block):
        rows = t_mm(pick, recv[got][...].reshape(16, 128))
        return mm_t(fold[0:8], jnp.where(block, rows, 0.0))

    pos0, lab0 = packets(tgt0[...], 13, 4, True)
    fill_packets("a1", pos0, lab0, 4, cpl0[...])
    Q0, V0 = bas0[:, 0:128], bas0[:, 128:256]
    t0 = mm(src0[...], Q0)
    loc0 = mm(src0[...], blk0[...])

    pl.semaphore_wait(barrier, greeted)
    share("x0a", "x", t0)
    start("a1", "zc")

    mh0, mc0 = mask_of(rnk0, leaf, 0), mask_of(rnk0, leaf, 1)
    V1 = bas1[:, 128:256]
    send["q_xc"][...] = t_mm(exp1[...], V1).reshape(8, 16, 128)
    hq0 = total("x0a", "x") * mh0
    y0 = loc0 + mm_t(hq0, exp0[...])
    share("x0b", "x", mm(y0, V0))
    start("q_xc", "xc")
    z0 = y0 * piv0[...]
    QW1 = chain(bas1[:, 0:128], blk1[...], V1)
    t1_src = mm(src1[...], QW1)
    share("w0", "zc", total("x0b", "x") * mc0)
    share("zp0", "x", mm(z0, exp0[...]))

    s_row = iota((256, 256), 0)
    r_col = iota((256, 256), 1)
    turn_a = ones_where(r_col == ((s_row >> 2) & 15) * 16 + (s_row >> 6) * 4 + (s_row & 3))
    wait("a1", "zc")
    moved = mm(turn_a, recv["a1"][:, 0:16, :].reshape(256, 128))
    send["a2"][:, 0:64, :] = moved.reshape(4, 64, 128)
    send["a2"][:, 64:80, :] = jnp.broadcast_to(recv["a1"][:, 16:17, :].reshape(1, 16, 128), (4, 16, 128))
    start("a2", "x")
    share("q_z", "z", total("q_xc", "xc"))

    pos1, lab1 = packets(tgt1[...], 14, 3, False)
    pick1, block1 = fill_packets("b1", pos1, lab1, 3, cpl1[...])
    pos2, lab2 = packets(tgt2[...], 15, 4, False)
    pick2, block2 = fill_packets("c1", pos2, lab2, 4, cpl2[...])
    V2 = bas2[:, 128:256]
    P3 = exp3[...]
    send["r_xc"][:, 0:16, :] = t_mm(exp2[...], V2).reshape(8, 16, 128)
    send["r_xc"][:, 16:32, :] = t_mm(P3, P3 * column(piv3[...])).reshape(8, 16, 128)

    front0 = (iota((128, 256), 0) >> 3) == ((iota((128, 256), 1) & 63) >> 2)
    spread4 = ones_where(iota((256, 64), 1) == (iota((256, 64), 0) >> 2))
    mine = iota((256, 128), 1) == x * 4 + (iota((256, 128), 0) & 3)
    wait("w0", "zc")
    wait("a2", "x")
    c0h = recv["a2"][:, 0:64, :].reshape(256, 128)
    e0 = jnp.where(front0, mm_t(recv["w0"][...].reshape(128, 128), c0h), 0.0)
    spread = mm(spread4, recv["a2"][:, 64:80, :].reshape(64, 128))
    lab_col = jnp.sum(jnp.where(mine, spread, 0.0), axis=1, keepdims=True)
    oh0 = ones_where(iota((256, 256), 1).astype(jnp.float32) == lab_col - 1.0)
    inc0 = -mm(jnp.sum(e0.reshape(16, 8, 256), axis=0), oh0)
    t1 = t1_src + mm(inc0[:, 0:128], QW1)
    share("f1_xc", "xc", jnp.concatenate([t1[:, 0:128], t1[:, 128:256]], axis=0))
    values_up("d1", inc0[:, 128:256], pick1, block1)
    start("b1", "zc")
    loc1 = mm(src1[...] + inc0[:, 0:128], blk1[...])
    ohq0 = mm(oh0[:, 0:128], QW1)

    share("f1_z", "z", total("f1_xc", "xc"))
    start("c1", "zc")
    start("r_xc", "xc")
    QW2 = chain(bas2[:, 0:128], blk2[...], V2)
    t2_src = mm(src2[...], QW2)
    share("q_g", "xc", total("q_z", "z"))
    wait("d1", "zc")
    values_on("d2", "d1", 8, 16, "k8")
    wait("b1", "zc")
    turn_b = ones_where(iota((128, 128), 1) == (iota((128, 128), 0) & 15) * 8 + (iota((128, 128), 0) >> 4))
    send["b2"][:, 0:16, :] = mm(turn_b, recv["b1"][:, 0:8, :].reshape(128, 128)).reshape(8, 16, 128)
    send["b2"][:, 16:32, :] = jnp.broadcast_to(recv["b1"][:, 8:9, :].reshape(1, 16, 128), (8, 16, 128))
    start("b2", "k8")
    share("r_z", "z", total("r_xc", "xc"))

    mh1, mc1 = mask_of(rnk1, y, 0), mask_of(rnk1, y, 1)
    wait("q_g", "xc")
    cr1 = recv["q_g"][...].reshape(128, 128)
    tot1 = total("f1_z", "z")
    hq1 = tot1[0:8] * mh1
    share("f1_y", "y2", (tot1[8:16] + mm(hq1, cr1)) * mc1)
    z1 = (loc1 + mm_t(hq1, exp1[...])) * piv1[...]
    zp1_own = mm(z1, exp1[...])
    zeta1 = mm_t(z1, blk1[...])

    wait("b2", "k8")
    c1h = recv["b2"][:, 0:16, :].reshape(128, 128)
    lab_in = recv["b2"][:, 16:32, :].reshape(128, 128)
    lab_col = jnp.sum(jnp.where(iota((128, 128), 1) == k8, lab_in, 0.0), axis=1, keepdims=True)
    oh1 = ones_where(iota((128, 256), 1).astype(jnp.float32) == lab_col - 1.0)
    ohq1 = mm(oh1[:, 0:128], QW2)
    kl1 = jnp.concatenate([t_mm(c1h[0:64], ohq1[0:64]), t_mm(c1h[64:128], ohq1[64:128])], axis=0)
    wait("d2", "k8")
    came1 = values_in("d2", 8)
    t2_src = t2_src + mm(came1, ohq1)
    inc1_came = mm(came1, oh1)
    wait("f1_y", "y2")
    w1 = recv["f1_y"]
    t2 = t2_src - mm(jnp.concatenate([w1[0], w1[1]], axis=1), kl1)
    share("f2_xc", "xc", jnp.concatenate([t2[:, 0:128], t2[:, 128:256], zp1_own], axis=0))
    front1 = (iota((16, 128), 0) >> 3) == (iota((16, 128), 1) >> 6)
    e1 = jnp.where(front1, mm_t(recv["f1_y"][...].reshape(16, 128), c1h), 0.0)
    inc1 = inc1_came - mm(e1[0:8] + e1[8:16], oh1)
    values_up("e1", inc1[:, 128:256], pick2, block2)
    loc2 = mm(src2[...] + inc1[:, 0:128], blk2[...])
    wait("c1", "zc")
    turn_c = ones_where(r_col == (s_row & 15) * 16 + (s_row >> 4))
    send["c2"][:, 0:16, :] = mm(turn_c, recv["c1"][:, 0:16, :].reshape(256, 128)).reshape(16, 16, 128)
    send["c2"][:, 16:32, :] = jnp.broadcast_to(recv["c1"][:, 16:17, :].reshape(1, 16, 128), (16, 16, 128))
    share("f2_z", "z", total("f2_xc", "xc"))
    start("c2", "k16")
    share("r_y", "y4", total("r_z", "z"))
    QW3 = chain(bas3[:, 0:128], blk3[...] * piv3[...], P3)
    t3_src = mm(src3[...], QW3)
    wait("e1", "zc")
    values_on("e2", "e1", 16, 16, "k16")
    wait("r_y", "y4")
    ry = recv["r_y"]
    share(
        "r_g",
        "xc",
        jnp.concatenate(
            [
                ry[0, 0:16, :] + ry[1, 0:16, :],
                ry[2, 0:16, :] + ry[3, 0:16, :],
                (ry[0, 16:32, :] + ry[1, 16:32, :]) + (ry[2, 16:32, :] + ry[3, 16:32, :]),
            ],
            axis=0,
        ),
    )
    share("f2_y", "y4", total("f2_z", "z"))
    wait("c2", "k16")
    c2h = recv["c2"][:, 0:16, :].reshape(256, 128)
    lab_in = recv["c2"][:, 16:32, :].reshape(256, 128)
    lab_col = jnp.sum(jnp.where(iota((256, 128), 1) == k16, lab_in, 0.0), axis=1, keepdims=True)
    oh2 = ones_where(iota((256, 128), 1).astype(jnp.float32) == lab_col - 1.0)
    ohq2 = mm(oh2, QW3)
    kl2 = jnp.concatenate([t_mm(c2h[0:128], ohq2[0:128]), t_mm(c2h[128:256], ohq2[128:256])], axis=0)
    wait("r_g", "xc")
    rg = recv["r_g"]
    cr2_each = [rg[:, 0:16, :].reshape(128, 128), rg[:, 16:32, :].reshape(128, 128)]
    m3 = rg[:, 32:48, :].reshape(128, 128)
    wait("f2_y", "y4")
    fy = recv["f2_y"]
    hq2_each, w2_each = [], []
    for v in range(2):
        t_q = fy[2 * v, 0:8, :] + fy[2 * v + 1, 0:8, :]
        t_v = fy[2 * v, 8:16, :] + fy[2 * v + 1, 8:16, :]
        hq = t_q * mask_of(rnk2, v, 0)
        hq2_each.append(hq)
        w2_each.append((t_v + mm(hq, cr2_each[v])) * mask_of(rnk2, v, 1))
    zp1 = fy[y, 16:24, :]
    first = u == 0
    hq2 = jnp.where(first, hq2_each[0], hq2_each[1])
    cr2 = jnp.where(first, cr2_each[0], cr2_each[1])
    mh2, mc2 = mask_of(rnk2, u, 0), mask_of(rnk2, u, 1)
    z2 = (loc2 + mm_t(hq2, exp2[...])) * piv2[...]
    zp2_own = mm(z2, exp2[...])

    t3_w = mm(jnp.concatenate(w2_each, axis=1), kl2)
    front2 = (iota((16, 256), 0) >> 3) == (iota((16, 256), 1) >> 7)
    wait("e2", "k16")
    came2 = values_in("e2", 16)
    t3 = t3_src + mm(came2, ohq2) - t3_w
    share("f3_xc", "xc", jnp.concatenate([t3[:, 0:128], t3[:, 128:256], zp2_own], axis=0))
    e2 = jnp.where(front2, mm_t(jnp.concatenate(w2_each, axis=0), c2h), 0.0)
    b3 = src3[...] + mm(came2 - (e2[0:8] + e2[8:16]), oh2)
    loc3 = mm(b3, blk3[...])
    share("f3_z", "z", total("f3_xc", "xc"))
    zeta3 = mm_t(loc3 * piv3[...], blk3[...])
    vals = mm_t(zeta3, oh2)
    u2_own = mm(jnp.where(front2, jnp.concatenate([vals, vals], axis=0), 0.0), c2h)
    zeta2 = mm_t(z2, blk2[...])
    mh3 = mask_of(rnk3, 0, 0)
    share("x0c", "x", t_mm(exp0[...], V0))
    share("f3_y", "y4", total("f3_z", "z"))
    QW0 = chain(Q0, blk0[...], V0)
    wait("f3_y", "y4")
    fy = recv["f3_y"]
    lower = fy[0] + fy[1]
    upper = fy[2] + fy[3]
    both = lower + upper
    hq3 = both[0:8] * mh3
    zp2 = jnp.where(first, lower[16:24], upper[16:24])
    g3 = (both[8:16] + mm(hq3, m3)) * mh3
    gh3 = jnp.concatenate([g3, hq3], axis=1)

    u2_low = mm_t(gh3, kl2)
    share("u2_xc", "xc", u2_own + jnp.concatenate([u2_low[:, 0:128], u2_low[:, 128:256]], axis=0))
    x3 = zeta3 + mm_t(gh3, QW3)
    out[3] = x3
    values_down("g1", oh2, x3, 16, "k16")
    share("u2_z", "z", total("u2_xc", "xc"))
    vals = mm_t(zeta2, oh1[:, 0:128])
    wait("g1", "k16")
    values_on("g2", "g1", 16, 16, "zc")
    share("u2_y", "y4", total("u2_z", "z"))
    wait("g2", "zc")
    xu2 = values_back("g2", pick2, block2)
    vals = vals + mm_t(xu2, oh1[:, 128:256])
    u1_own = mm(jnp.where(front1, jnp.concatenate([vals, vals], axis=0), 0.0), c1h)
    s2_all = total("u2_y", "y4")
    s2 = jnp.where(first, s2_all[0:8], s2_all[8:16]) * mc2
    g2 = (zp2 - mm_t(s2, cr2)) * mh2
    gs2 = jnp.concatenate([g2, -s2], axis=1)

    u1_low = mm_t(gs2, kl1)
    share("u1_xc", "xc", u1_own + jnp.concatenate([u1_low[:, 0:128], u1_low[:, 128:256]], axis=0))
    x2 = zeta2 + mm_t(gs2, QW2)
    out[2] = x2
    values_down("h1", oh1, jnp.concatenate([x2, xu2], axis=1), 8, "k8")
    share("u1_z", "z", total("u1_xc", "xc"))
    vals = mm_t(zeta1, oh0[:, 0:128])
    cr0 = total("x0c", "x")
    zp0 = total("zp0", "x")
    zeta0 = mm_t(z0, blk0[...])
    wait("h1", "k8")
    values_on("h2", "h1", 16, 8, "zc")
    share("u1_y", "y2", total("u1_z", "z"))
    wait("h2", "zc")
    xu1 = values_back("h2", pick1, block1)
    vals = vals + mm_t(xu1, oh0[:, 128:256])
    s1_all = total("u1_y", "y2")
    s1 = jnp.where(yb == 0, s1_all[0:8], s1_all[8:16]) * mc1
    g1 = (zp1 - mm_t(s1, cr1)) * mh1
    gs1 = jnp.concatenate([g1, -s1], axis=1)

    vals = vals + mm_t(gs1, ohq0)
    send["u0_zc"][...] = mm(jnp.where(front0, stack16(vals), 0.0), c0h).reshape(16, 8, 128)
    start("u0_zc", "zc")
    out[1] = zeta1 + mm_t(gs1, QW1)
    share("u0_x", "x", total("u0_zc", "zc"))
    s0 = total("u0_x", "x") * mc0
    g0 = (zp0 - mm_t(s0, cr0)) * mh0
    out[0] = zeta0 + mm_t(jnp.concatenate([g0, -s0], axis=1), QW0)

    for name, axis in pending:
        whole(name, axis).wait_send()


def apart(answers, *refs):
    copies = [pltpu.make_async_copy(answers.at[k], refs[k], refs[4].at[k]) for k in range(4)]
    for copy in copies:
        copy.start()
    for copy in copies:
        copy.wait()


def shards(*args):
    args = list(args)
    for i in (4, 12, 20, 28):
        args[i] = args[i].reshape(1, -1)
    for i in (7, 15, 23):
        args[i] = args[i].reshape(1, -1)
    for i in (6, 14):
        args[i] = args[i].T
    hbm = pl.BlockSpec(memory_space=pltpu.HBM)
    vmem = pl.BlockSpec(memory_space=pltpu.VMEM)
    sizes = {name: (n, rows, 128) for name, n, rows, _ in EXCHANGES}
    scratch = [pltpu.VMEM(arg.shape, arg.dtype) for arg in args]
    scratch += [pltpu.VMEM(sizes[name], jnp.float32) for name in NAMES]
    scratch += [pltpu.VMEM(sizes[name], jnp.float32) for name in SCATTERED]
    scratch += [pltpu.SemaphoreType.DMA((len(NAMES),)), pltpu.SemaphoreType.DMA((len(NAMES),))]
    scratch += [pltpu.SemaphoreType.DMA((len(args),))]
    answers = pl.pallas_call(
        kernel,
        out_shape=jax.ShapeDtypeStruct((4, 8, 128), jnp.float32),
        in_specs=[hbm] * len(args),
        out_specs=vmem,
        scratch_shapes=scratch,
        compiler_params=pltpu.CompilerParams(
            collective_id=0, has_side_effects=True, vmem_limit_bytes=67043328
        ),
        name="solve",
    )(*args)
    return tuple(
        pl.pallas_call(
            apart,
            out_shape=[jax.ShapeDtypeStruct((8, 128), jnp.float32)] * 4,
            in_specs=[vmem],
            out_specs=[hbm] * 4,
            scratch_shapes=[pltpu.SemaphoreType.DMA((4,))],
            name="apart",
        )(answers)
    )


def solution(mesh):
    columns = P(None, ("leaf", "grid"))
    rows = P(("leaf", "grid"), None)
    flat = P(("leaf", "grid"))
    level = (columns, rows, rows, rows, flat, rows, P(), flat)
    in_specs = level * 3 + (columns, rows, rows, rows, flat, P())
    return jax.shard_map(
        shards, mesh=mesh, in_specs=in_specs, out_specs=(columns,) * 4, check_vma=False
    )
```

time: 111 us -> 105 us (0.946)
  Pallas kernels: 110 us -> 104 us
    pallas_call x1, Pallas kernels: 109 us -> 103 us  [shards(): pl.pallas_call(kernel, out_shape=jax.ShapeDtypeStruct((4, 8, 128), jnp.fl...]
where the time goes in v2:
time: 105 us
  Pallas kernels  104 us (99%)
    pallas_call x1, Pallas kernels, shards(): pl.pallas_call(kernel, out_shape=jax.ShapeDtypeStruct((4, 8, 128), jnp.fl...  103 us

profile of v2, /device:TPU:1, one launch (start us, length us, event | category | flops | bytes accessed | tf_op | source)
XLA Modules:
  0.0 104.6 jit_solution(130313222816010730)
XLA Ops:
  0.6 102.5 %solve.1.answers = f32[4,8,128]{2,1,0:T(8,128)} custom-call(f32[8,128]{1,0:T(8,128)} %refs_0_.1, f32[128,128]{1,0:T(8,128)} %refs_1_.1, f32[128,128]{1,0:T(8,128)} %refs_2_.1, f32[128,256]{1,0:T(8,128)} %refs_3_.1, f32[1,128]{1,0:T(1,128)} %bitcast.12, f32[256,128]{1,0:T(8,128)} %refs_5_.1, s32[2,64]{1,0:T(2,128)} %bitcast.9, s32[1,256]{1,0:T(1,128)} %bitcast.10, ...), custom_call_target="tpu_custom_call" | custom-call | tf_op jit(solution)/shard_map/solve/pallas_call | solution.py:571
  103.2 1.4 %apart.1 = (f32[8,128]{1,0:T(8,128)}, f32[8,128]{1,0:T(8,128)}, f32[8,128]{1,0:T(8,128)}, f32[8,128]{1,0:T(8,128)}) custom-call(f32[4,8,128]{2,1,0:T(8,128)} %solve.1.answers), custom_call_target="tpu_custom_call" | custom-call | tf_op jit(solution)/shard_map/apart/pallas_call | solution.py:583

commit v3 on v2

--- a/solution.py
+++ b/solution.py
@@ -8,7 +8,7 @@
 from jax.sharding import PartitionSpec as P
 
 MESH = pl.DeviceIdType.MESH
-HIGHEST = lax.Precision.HIGHEST
+PRECISION = lax.Precision.HIGH
 
 NX, NZC, NY = 4, 16, 4
 
@@ -34,19 +34,24 @@
     ("f1_xc", 8, 16, 16),
     ("f1_z", 8, 16, 16),
     ("f1_y", 2, 8, 8),
-    ("f2_xc", 8, 24, 24),
-    ("f2_z", 8, 24, 24),
-    ("f2_y", 4, 24, 24),
-    ("f3_xc", 8, 24, 24),
-    ("f3_z", 8, 24, 24),
-    ("f3_y", 4, 24, 24),
+    ("f2_xc", 8, 16, 16),
+    ("f2_z", 8, 16, 16),
+    ("f2_y", 4, 16, 16),
+    ("f3_c", 2, 8, 8),
+    ("f3_k", 16, 8, 8),
+    ("f3_z", 8, 8, 8),
+    ("f3_g", 2, 8, 8),
+    ("zp_xc", 8, 16, 16),
+    ("zp_z", 8, 16, 16),
+    ("zp_y", 2, 8, 8),
     ("d1", 16, 1, 1),
     ("d2", 8, 1, 1),
     ("e1", 16, 1, 1),
     ("e2", 16, 1, 1),
-    ("u2_xc", 8, 16, 16),
-    ("u2_z", 8, 16, 16),
-    ("u2_y", 4, 16, 16),
+    ("u2_c", 2, 8, 8),
+    ("u2_k", 16, 8, 8),
+    ("u2_z", 8, 8, 8),
+    ("u2_g", 2, 8, 8),
     ("g1", 16, 1, 1),
     ("g2", 16, 1, 1),
     ("u1_xc", 8, 16, 16),
@@ -60,13 +65,13 @@
 NAMES = [entry[0] for entry in EXCHANGES]
 SENT = {entry[0]: entry[3] for entry in EXCHANGES}
 SCATTERED = [
-    "a1", "a2", "b1", "b2", "c1", "c2", "q_xc", "r_xc", "d1", "d2", "e1", "e2", "g1", "g2", "h1", "h2", "u0_zc"
+    "a1", "a2", "b1", "b2", "c1", "c2", "q_xc", "r_xc", "d1", "d2", "e1", "e2", "f3_c", "u2_c", "g1", "g2", "h1", "h2", "u0_zc"
 ]
 
 
 def dot(a, b, ca, cb):
     return lax.dot_general(
-        a, b, (((ca,), (cb,)), ((), ())), precision=HIGHEST, preferred_element_type=jnp.float32
+        a, b, (((ca,), (cb,)), ((), ())), precision=PRECISION, preferred_element_type=jnp.float32
     )
 
 
@@ -151,6 +156,7 @@
         "x": (x, 4, lambda d: (leaf, d)),
         "zc": (zc, 16, lambda d: (y * 16 + d, x)),
         "xc": (xc, 8, lambda d: (leaf - c + d % 2, d // 2)),
+        "c": (c, 2, lambda d: (leaf - c + d, x)),
         "z": (z, 8, lambda d: (y * 16 + d * 2 + c, x)),
         "y2": (yb, 2, lambda d: ((u * 2 + d) * 16 + zc, x)),
         "y4": (y, 4, lambda d: (d * 16 + zc, x)),
@@ -202,6 +208,11 @@
     def total(name, axis):
         wait(name, axis)
         return jnp.sum(recv[name][...], axis=0)
+
+    def scatter_halves(name, low, high):
+        send[name][0] = low
+        send[name][1] = high
+        start(name, "c")
 
     barrier = pltpu.get_barrier_semaphore()
 
@@ -377,6 +388,9 @@
     send["b2"][:, 0:16, :] = mm(turn_b, recv["b1"][:, 0:8, :].reshape(128, 128)).reshape(8, 16, 128)
     send["b2"][:, 16:32, :] = jnp.broadcast_to(recv["b1"][:, 8:9, :].reshape(1, 16, 128), (8, 16, 128))
     start("b2", "k8")
+    QW3 = chain(bas3[:, 0:128], blk3[...] * piv3[...], P3)
+    t3_src = mm(src3[...], QW3)
+    turn_c = ones_where(r_col == (s_row & 15) * 16 + (s_row >> 4))
     share("r_z", "z", total("r_xc", "xc"))
 
     mh1, mc1 = mask_of(rnk1, y, 0), mask_of(rnk1, y, 1)
@@ -403,21 +417,18 @@
     wait("f1_y", "y2")
     w1 = recv["f1_y"]
     t2 = t2_src - mm(jnp.concatenate([w1[0], w1[1]], axis=1), kl1)
-    share("f2_xc", "xc", jnp.concatenate([t2[:, 0:128], t2[:, 128:256], zp1_own], axis=0))
+    share("f2_xc", "xc", jnp.concatenate([t2[:, 0:128], t2[:, 128:256]], axis=0))
     front1 = (iota((16, 128), 0) >> 3) == (iota((16, 128), 1) >> 6)
     e1 = jnp.where(front1, mm_t(recv["f1_y"][...].reshape(16, 128), c1h), 0.0)
     inc1 = inc1_came - mm(e1[0:8] + e1[8:16], oh1)
     values_up("e1", inc1[:, 128:256], pick2, block2)
     loc2 = mm(src2[...] + inc1[:, 0:128], blk2[...])
     wait("c1", "zc")
-    turn_c = ones_where(r_col == (s_row & 15) * 16 + (s_row >> 4))
     send["c2"][:, 0:16, :] = mm(turn_c, recv["c1"][:, 0:16, :].reshape(256, 128)).reshape(16, 16, 128)
     send["c2"][:, 16:32, :] = jnp.broadcast_to(recv["c1"][:, 16:17, :].reshape(1, 16, 128), (16, 16, 128))
-    share("f2_z", "z", total("f2_xc", "xc"))
     start("c2", "k16")
     share("r_y", "y4", total("r_z", "z"))
-    QW3 = chain(bas3[:, 0:128], blk3[...] * piv3[...], P3)
-    t3_src = mm(src3[...], QW3)
+    share("f2_z", "z", total("f2_xc", "xc"))
     wait("e1", "zc")
     values_on("e2", "e1", 16, 16, "k16")
     wait("r_y", "y4")
@@ -455,7 +466,6 @@
         hq = t_q * mask_of(rnk2, v, 0)
         hq2_each.append(hq)
         w2_each.append((t_v + mm(hq, cr2_each[v])) * mask_of(rnk2, v, 1))
-    zp1 = fy[y, 16:24, :]
     first = u == 0
     hq2 = jnp.where(first, hq2_each[0], hq2_each[1])
     cr2 = jnp.where(first, cr2_each[0], cr2_each[1])
@@ -468,45 +478,49 @@
     wait("e2", "k16")
     came2 = values_in("e2", 16)
     t3 = t3_src + mm(came2, ohq2) - t3_w
-    share("f3_xc", "xc", jnp.concatenate([t3[:, 0:128], t3[:, 128:256], zp2_own], axis=0))
+    scatter_halves("f3_c", t3[:, 0:128], t3[:, 128:256])
+    share("zp_xc", "xc", jnp.concatenate([zp1_own, zp2_own], axis=0))
+    share("f3_k", "k16", total("f3_c", "c"))
     e2 = jnp.where(front2, mm_t(jnp.concatenate(w2_each, axis=0), c2h), 0.0)
     b3 = src3[...] + mm(came2 - (e2[0:8] + e2[8:16]), oh2)
     loc3 = mm(b3, blk3[...])
-    share("f3_z", "z", total("f3_xc", "xc"))
     zeta3 = mm_t(loc3 * piv3[...], blk3[...])
     vals = mm_t(zeta3, oh2)
     u2_own = mm(jnp.where(front2, jnp.concatenate([vals, vals], axis=0), 0.0), c2h)
+    share("f3_z", "z", total("f3_k", "k16"))
     zeta2 = mm_t(z2, blk2[...])
     mh3 = mask_of(rnk3, 0, 0)
+    zp_sum = total("zp_xc", "xc")
+    QW0 = chain(Q0, blk0[...], V0)
+    share("f3_g", "c", total("f3_z", "z"))
+    share("zp_z", "z", zp_sum)
+    wait("f3_g", "c")
+    hq3 = recv["f3_g"][0] * mh3
+    g3 = (recv["f3_g"][1] + mm(hq3, m3)) * mh3
+    gh3 = jnp.concatenate([g3, hq3], axis=1)
+
+    u2_low = mm_t(gh3, kl2)
+    scatter_halves("u2_c", u2_own[0:8] + u2_low[:, 0:128], u2_own[8:16] + u2_low[:, 128:256])
+    x3 = zeta3 + mm_t(gh3, QW3)
+    share("u2_k", "k16", total("u2_c", "c"))
+    values_down("g1", oh2, x3, 16, "k16")
+    out[3] = x3
+    vals = mm_t(zeta2, oh1[:, 0:128])
     share("x0c", "x", t_mm(exp0[...], V0))
-    share("f3_y", "y4", total("f3_z", "z"))
-    QW0 = chain(Q0, blk0[...], V0)
-    wait("f3_y", "y4")
-    fy = recv["f3_y"]
-    lower = fy[0] + fy[1]
-    upper = fy[2] + fy[3]
-    both = lower + upper
-    hq3 = both[0:8] * mh3
-    zp2 = jnp.where(first, lower[16:24], upper[16:24])
-    g3 = (both[8:16] + mm(hq3, m3)) * mh3
-    gh3 = jnp.concatenate([g3, hq3], axis=1)
-
-    u2_low = mm_t(gh3, kl2)
-    share("u2_xc", "xc", u2_own + jnp.concatenate([u2_low[:, 0:128], u2_low[:, 128:256]], axis=0))
-    x3 = zeta3 + mm_t(gh3, QW3)
-    out[3] = x3
-    values_down("g1", oh2, x3, 16, "k16")
-    share("u2_z", "z", total("u2_xc", "xc"))
-    vals = mm_t(zeta2, oh1[:, 0:128])
+    share("u2_z", "z", total("u2_k", "k16"))
     wait("g1", "k16")
     values_on("g2", "g1", 16, 16, "zc")
-    share("u2_y", "y4", total("u2_z", "z"))
+    zp_sum = total("zp_z", "z")
+    zp1 = zp_sum[0:8]
+    share("zp_y", "y2", zp_sum[8:16])
+    share("u2_g", "c", total("u2_z", "z"))
+    zp2 = total("zp_y", "y2")
     wait("g2", "zc")
     xu2 = values_back("g2", pick2, block2)
     vals = vals + mm_t(xu2, oh1[:, 128:256])
     u1_own = mm(jnp.where(front1, jnp.concatenate([vals, vals], axis=0), 0.0), c1h)
-    s2_all = total("u2_y", "y4")
-    s2 = jnp.where(first, s2_all[0:8], s2_all[8:16]) * mc2
+    wait("u2_g", "c")
+    s2 = recv["u2_g"][u] * mc2
     g2 = (zp2 - mm_t(s2, cr2)) * mh2
     gs2 = jnp.concatenate([g2, -s2], axis=1)
 
@@ -583,7 +597,7 @@
         pl.pallas_call(
             apart,
             out_shape=[jax.ShapeDtypeStruct((8, 128), jnp.float32)] * 4,
-            in_specs=[vmem],
+            in_specs=[hbm],
             out_specs=[hbm] * 4,
             scratch_shapes=[pltpu.SemaphoreType.DMA((4,))],
             name="apart",

time: 105 us -> 98.6 us (0.939)
  Pallas kernels: 104 us -> 97.6 us
    pallas_call x1, Pallas kernels: 103 us -> 96 us  [shards(): pl.pallas_call(kernel, out_shape=jax.ShapeDtypeStruct((4, 8, 128), jnp.fl...]
where the time goes in v3:
time: 98.6 us; the launch traced here: 98.3 us
  Pallas kernels  97.6 us (99%)
    pallas_call x1, Pallas kernels, shards(): pl.pallas_call(kernel, out_shape=jax.ShapeDtypeStruct((4, 8, 128), jnp.fl...  96 us

profile of v3, /device:TPU:1, one launch (start us, length us, event | category | flops | bytes accessed | tf_op | source)
XLA Modules:
  0.0 98.3 jit_solution(2156773968038007533)
XLA Ops:
  0.6 96.0 %solve.1.answers = f32[4,8,128]{2,1,0:T(8,128)} custom-call(f32[8,128]{1,0:T(8,128)} %refs_0_.1, f32[128,128]{1,0:T(8,128)} %refs_1_.1, f32[128,128]{1,0:T(8,128)} %refs_2_.1, f32[128,256]{1,0:T(8,128)} %refs_3_.1, f32[1,128]{1,0:T(1,128)} %bitcast.12, f32[256,128]{1,0:T(8,128)} %refs_5_.1, s32[2,64]{1,0:T(2,128)} %bitcast.9, s32[1,256]{1,0:T(1,128)} %bitcast.10, ...), custom_call_target="tpu_custom_call" | custom-call | tf_op jit(solution)/shard_map/solve/pallas_call | solution.py:585
  96.6 1.6 %apart.1 = (f32[8,128]{1,0:T(8,128)}, f32[8,128]{1,0:T(8,128)}, f32[8,128]{1,0:T(8,128)}, f32[8,128]{1,0:T(8,128)}) custom-call(f32[4,8,128]{2,1,0:T(8,128)} %solve.1.answers), custom_call_target="tpu_custom_call" | custom-call | tf_op jit(solution)/shard_map/apart/pallas_call | solution.py:597

commit v4 on v3

--- a/solution.py
+++ b/solution.py
@@ -8,7 +8,8 @@
 from jax.sharding import PartitionSpec as P
 
 MESH = pl.DeviceIdType.MESH
-PRECISION = lax.Precision.HIGH
+HIGH = lax.Precision.HIGH
+HIGHEST = lax.Precision.HIGHEST
 
 NX, NZC, NY = 4, 16, 4
 
@@ -19,11 +20,11 @@
     ("zp0", 4, 8, 8),
     ("w0", 16, 8, 8),
     ("a1", 16, 24, 17),
-    ("a2", 4, 80, 80),
+    ("a2", 4, 72, 72),
     ("b1", 16, 16, 9),
-    ("b2", 8, 32, 32),
+    ("b2", 8, 24, 17),
     ("c1", 16, 24, 17),
-    ("c2", 16, 32, 32),
+    ("c2", 16, 24, 17),
     ("q_xc", 8, 16, 16),
     ("q_z", 8, 16, 16),
     ("q_g", 8, 16, 16),
@@ -34,9 +35,10 @@
     ("f1_xc", 8, 16, 16),
     ("f1_z", 8, 16, 16),
     ("f1_y", 2, 8, 8),
-    ("f2_xc", 8, 16, 16),
+    ("f2_c", 2, 8, 8),
+    ("f2_k", 16, 8, 8),
     ("f2_z", 8, 16, 16),
-    ("f2_y", 4, 16, 16),
+    ("f2_g", 2, 16, 16),
     ("f3_c", 2, 8, 8),
     ("f3_k", 16, 8, 8),
     ("f3_z", 8, 8, 8),
@@ -54,9 +56,10 @@
     ("u2_g", 2, 8, 8),
     ("g1", 16, 1, 1),
     ("g2", 16, 1, 1),
-    ("u1_xc", 8, 16, 16),
-    ("u1_z", 8, 16, 16),
-    ("u1_y", 2, 16, 16),
+    ("u1_c", 2, 8, 8),
+    ("u1_k", 8, 8, 8),
+    ("u1_z", 8, 8, 8),
+    ("u1_g", 2, 8, 8),
     ("h1", 8, 1, 1),
     ("h2", 16, 1, 1),
     ("u0_zc", 16, 8, 8),
@@ -65,26 +68,26 @@
 NAMES = [entry[0] for entry in EXCHANGES]
 SENT = {entry[0]: entry[3] for entry in EXCHANGES}
 SCATTERED = [
-    "a1", "a2", "b1", "b2", "c1", "c2", "q_xc", "r_xc", "d1", "d2", "e1", "e2", "f3_c", "u2_c", "g1", "g2", "h1", "h2", "u0_zc"
+    "a1", "a2", "b1", "b2", "c1", "c2", "q_xc", "r_xc", "d1", "d2", "e1", "e2", "f2_c", "f3_c", "u2_c", "u1_c", "g1", "g2", "h1", "h2", "u0_zc"
 ]
 
 
-def dot(a, b, ca, cb):
+def dot(a, b, ca, cb, precision):
     return lax.dot_general(
-        a, b, (((ca,), (cb,)), ((), ())), precision=PRECISION, preferred_element_type=jnp.float32
+        a, b, (((ca,), (cb,)), ((), ())), precision=precision, preferred_element_type=jnp.float32
     )
 
 
-def mm(a, b):
-    return dot(a, b, 1, 0)
-
-
-def mm_t(a, b):
-    return dot(a, b, 1, 1)
-
-
-def t_mm(a, b):
-    return dot(a, b, 0, 0)
+def mm(a, b, precision=HIGH):
+    return dot(a, b, 1, 0, precision)
+
+
+def mm_t(a, b, precision=HIGH):
+    return dot(a, b, 1, 1, precision)
+
+
+def t_mm(a, b, precision=HIGH):
+    return dot(a, b, 0, 0, precision)
 
 
 def iota(shape, dim):
@@ -270,7 +273,7 @@
     def fill_packets(name, pos, label, kbits, couple):
         k = 1 << kbits
         n = pos.shape[1]
-        send[name][:, 0:k, :] = mm(place(pos, 16 * k), couple).reshape(16, k, 128)
+        send[name][:, 0:k, :] = mm(place(pos, 16 * k), couple, HIGHEST).reshape(16, k, 128)
         major, minor = halves(pos, kbits)
         pick = ones_where(iota((16, n), 0).astype(jnp.float32) == major)
         minor_col = column(minor)
@@ -280,7 +283,16 @@
         return pick, (iota((n, 128), 1) >> 3).astype(jnp.float32) == minor_col
 
     def chain(qv, w, p):
-        return jnp.concatenate([qv, mm(w, p)], axis=1)
+        return jnp.concatenate([qv, mm(w, p, HIGHEST)], axis=1)
+
+    def label_rows(name, row, count, packet):
+        labels = recv[name][:, row : row + 1, :].reshape(16, 128)
+        labels = jnp.concatenate([labels, jnp.zeros((112, 128), jnp.float32)], axis=0)
+        return mm_t(ones_where(iota((count, 128), 1) == packet(iota((count, 128), 0))), labels)
+
+    def label_column(rows, bits):
+        mine = iota(rows.shape, 1) == ((iota(rows.shape, 0) >> bits) & 15)
+        return jnp.sum(jnp.where(mine, rows, 0.0), axis=1, keepdims=True)
 
     fold = ones_where((iota((128, 128), 0) & 7) == (iota((128, 128), 1) & 7))
 
@@ -318,8 +330,8 @@
     pos0, lab0 = packets(tgt0[...], 13, 4, True)
     fill_packets("a1", pos0, lab0, 4, cpl0[...])
     Q0, V0 = bas0[:, 0:128], bas0[:, 128:256]
-    t0 = mm(src0[...], Q0)
-    loc0 = mm(src0[...], blk0[...])
+    t0 = mm(src0[...], Q0, HIGHEST)
+    loc0 = mm(src0[...], blk0[...], HIGHEST)
 
     pl.semaphore_wait(barrier, greeted)
     share("x0a", "x", t0)
@@ -327,26 +339,26 @@
 
     mh0, mc0 = mask_of(rnk0, leaf, 0), mask_of(rnk0, leaf, 1)
     V1 = bas1[:, 128:256]
-    send["q_xc"][...] = t_mm(exp1[...], V1).reshape(8, 16, 128)
+    send["q_xc"][...] = t_mm(exp1[...], V1, HIGHEST).reshape(8, 16, 128)
     hq0 = total("x0a", "x") * mh0
-    y0 = loc0 + mm_t(hq0, exp0[...])
+    y0 = loc0 + mm_t(hq0, exp0[...], HIGHEST)
     share("x0b", "x", mm(y0, V0))
     start("q_xc", "xc")
     z0 = y0 * piv0[...]
     QW1 = chain(bas1[:, 0:128], blk1[...], V1)
-    t1_src = mm(src1[...], QW1)
+    t1_src = mm(src1[...], QW1, HIGHEST)
     share("w0", "zc", total("x0b", "x") * mc0)
-    share("zp0", "x", mm(z0, exp0[...]))
+    share("zp0", "x", mm(z0, exp0[...], HIGHEST))
 
     s_row = iota((256, 256), 0)
     r_col = iota((256, 256), 1)
     turn_a = ones_where(r_col == ((s_row >> 2) & 15) * 16 + (s_row >> 6) * 4 + (s_row & 3))
     wait("a1", "zc")
-    moved = mm(turn_a, recv["a1"][:, 0:16, :].reshape(256, 128))
+    moved = mm(turn_a, recv["a1"][:, 0:16, :].reshape(256, 128), HIGHEST)
     send["a2"][:, 0:64, :] = moved.reshape(4, 64, 128)
-    send["a2"][:, 64:80, :] = jnp.broadcast_to(recv["a1"][:, 16:17, :].reshape(1, 16, 128), (4, 16, 128))
+    send["a2"][:, 64:72, :] = label_rows("a1", 16, 32, lambda r: (r >> 3) * 4 + (r & 3)).reshape(4, 8, 128)
     start("a2", "x")
-    share("q_z", "z", total("q_xc", "xc"))
+    q_sum = total("q_xc", "xc")
 
     pos1, lab1 = packets(tgt1[...], 14, 3, False)
     pick1, block1 = fill_packets("b1", pos1, lab1, 3, cpl1[...])
@@ -354,44 +366,42 @@
     pick2, block2 = fill_packets("c1", pos2, lab2, 4, cpl2[...])
     V2 = bas2[:, 128:256]
     P3 = exp3[...]
-    send["r_xc"][:, 0:16, :] = t_mm(exp2[...], V2).reshape(8, 16, 128)
-    send["r_xc"][:, 16:32, :] = t_mm(P3, P3 * column(piv3[...])).reshape(8, 16, 128)
+    send["r_xc"][:, 0:16, :] = t_mm(exp2[...], V2, HIGHEST).reshape(8, 16, 128)
+    send["r_xc"][:, 16:32, :] = t_mm(P3, P3 * column(piv3[...]), HIGHEST).reshape(8, 16, 128)
 
     front0 = (iota((128, 256), 0) >> 3) == ((iota((128, 256), 1) & 63) >> 2)
-    spread4 = ones_where(iota((256, 64), 1) == (iota((256, 64), 0) >> 2))
-    mine = iota((256, 128), 1) == x * 4 + (iota((256, 128), 0) & 3)
     wait("w0", "zc")
+    share("q_z", "z", q_sum)
     wait("a2", "x")
     c0h = recv["a2"][:, 0:64, :].reshape(256, 128)
     e0 = jnp.where(front0, mm_t(recv["w0"][...].reshape(128, 128), c0h), 0.0)
-    spread = mm(spread4, recv["a2"][:, 64:80, :].reshape(64, 128))
-    lab_col = jnp.sum(jnp.where(mine, spread, 0.0), axis=1, keepdims=True)
+    slots = recv["a2"][:, 64:72, :]
+    lab_col = label_column(jnp.concatenate([slots[v] for v in range(4) for _ in range(8)], axis=0), 2)
     oh0 = ones_where(iota((256, 256), 1).astype(jnp.float32) == lab_col - 1.0)
     inc0 = -mm(jnp.sum(e0.reshape(16, 8, 256), axis=0), oh0)
     t1 = t1_src + mm(inc0[:, 0:128], QW1)
     share("f1_xc", "xc", jnp.concatenate([t1[:, 0:128], t1[:, 128:256]], axis=0))
     values_up("d1", inc0[:, 128:256], pick1, block1)
     start("b1", "zc")
-    loc1 = mm(src1[...] + inc0[:, 0:128], blk1[...])
-    ohq0 = mm(oh0[:, 0:128], QW1)
+    loc1 = mm(src1[...] + inc0[:, 0:128], blk1[...], HIGHEST)
+    ohq0 = mm(oh0[:, 0:128], QW1, HIGHEST)
 
     share("f1_z", "z", total("f1_xc", "xc"))
+    share("q_g", "xc", total("q_z", "z"))
+    start("r_xc", "xc")
     start("c1", "zc")
-    start("r_xc", "xc")
     QW2 = chain(bas2[:, 0:128], blk2[...], V2)
-    t2_src = mm(src2[...], QW2)
-    share("q_g", "xc", total("q_z", "z"))
+    t2_src = mm(src2[...], QW2, HIGHEST)
     wait("d1", "zc")
     values_on("d2", "d1", 8, 16, "k8")
     wait("b1", "zc")
     turn_b = ones_where(iota((128, 128), 1) == (iota((128, 128), 0) & 15) * 8 + (iota((128, 128), 0) >> 4))
-    send["b2"][:, 0:16, :] = mm(turn_b, recv["b1"][:, 0:8, :].reshape(128, 128)).reshape(8, 16, 128)
-    send["b2"][:, 16:32, :] = jnp.broadcast_to(recv["b1"][:, 8:9, :].reshape(1, 16, 128), (8, 16, 128))
+    send["b2"][:, 0:16, :] = mm(turn_b, recv["b1"][:, 0:8, :].reshape(128, 128), HIGHEST).reshape(8, 16, 128)
+    send["b2"][:, 16:17, :] = label_rows("b1", 8, 8, lambda r: r).reshape(8, 1, 128)
     start("b2", "k8")
     QW3 = chain(bas3[:, 0:128], blk3[...] * piv3[...], P3)
-    t3_src = mm(src3[...], QW3)
+    t3_src = mm(src3[...], QW3, HIGHEST)
     turn_c = ones_where(r_col == (s_row & 15) * 16 + (s_row >> 4))
-    share("r_z", "z", total("r_xc", "xc"))
 
     mh1, mc1 = mask_of(rnk1, y, 0), mask_of(rnk1, y, 1)
     wait("q_g", "xc")
@@ -399,17 +409,17 @@
     tot1 = total("f1_z", "z")
     hq1 = tot1[0:8] * mh1
     share("f1_y", "y2", (tot1[8:16] + mm(hq1, cr1)) * mc1)
-    z1 = (loc1 + mm_t(hq1, exp1[...])) * piv1[...]
-    zp1_own = mm(z1, exp1[...])
-    zeta1 = mm_t(z1, blk1[...])
+    share("r_z", "z", total("r_xc", "xc"))
+    z1 = (loc1 + mm_t(hq1, exp1[...], HIGHEST)) * piv1[...]
+    zp1_own = mm(z1, exp1[...], HIGHEST)
+    zeta1 = mm_t(z1, blk1[...], HIGHEST)
 
     wait("b2", "k8")
     c1h = recv["b2"][:, 0:16, :].reshape(128, 128)
-    lab_in = recv["b2"][:, 16:32, :].reshape(128, 128)
-    lab_col = jnp.sum(jnp.where(iota((128, 128), 1) == k8, lab_in, 0.0), axis=1, keepdims=True)
+    lab_col = label_column(jnp.broadcast_to(recv["b2"][:, 16:17, :], (8, 16, 128)).reshape(128, 128), 0)
     oh1 = ones_where(iota((128, 256), 1).astype(jnp.float32) == lab_col - 1.0)
-    ohq1 = mm(oh1[:, 0:128], QW2)
-    kl1 = jnp.concatenate([t_mm(c1h[0:64], ohq1[0:64]), t_mm(c1h[64:128], ohq1[64:128])], axis=0)
+    ohq1 = mm(oh1[:, 0:128], QW2, HIGHEST)
+    kl1 = jnp.concatenate([t_mm(c1h[0:64], ohq1[0:64], HIGHEST), t_mm(c1h[64:128], ohq1[64:128], HIGHEST)], axis=0)
     wait("d2", "k8")
     came1 = values_in("d2", 8)
     t2_src = t2_src + mm(came1, ohq1)
@@ -417,18 +427,21 @@
     wait("f1_y", "y2")
     w1 = recv["f1_y"]
     t2 = t2_src - mm(jnp.concatenate([w1[0], w1[1]], axis=1), kl1)
-    share("f2_xc", "xc", jnp.concatenate([t2[:, 0:128], t2[:, 128:256]], axis=0))
+    scatter_halves("f2_c", t2[:, 0:128], t2[:, 128:256])
     front1 = (iota((16, 128), 0) >> 3) == (iota((16, 128), 1) >> 6)
     e1 = jnp.where(front1, mm_t(recv["f1_y"][...].reshape(16, 128), c1h), 0.0)
     inc1 = inc1_came - mm(e1[0:8] + e1[8:16], oh1)
+    share("f2_k", "k16", total("f2_c", "c"))
     values_up("e1", inc1[:, 128:256], pick2, block2)
-    loc2 = mm(src2[...] + inc1[:, 0:128], blk2[...])
+    share("r_y", "y4", total("r_z", "z"))
+    loc2 = mm(src2[...] + inc1[:, 0:128], blk2[...], HIGHEST)
     wait("c1", "zc")
-    send["c2"][:, 0:16, :] = mm(turn_c, recv["c1"][:, 0:16, :].reshape(256, 128)).reshape(16, 16, 128)
-    send["c2"][:, 16:32, :] = jnp.broadcast_to(recv["c1"][:, 16:17, :].reshape(1, 16, 128), (16, 16, 128))
+    send["c2"][:, 0:16, :] = mm(turn_c, recv["c1"][:, 0:16, :].reshape(256, 128), HIGHEST).reshape(16, 16, 128)
+    send["c2"][:, 16:17, :] = label_rows("c1", 16, 16, lambda r: r).reshape(16, 1, 128)
     start("c2", "k16")
-    share("r_y", "y4", total("r_z", "z"))
-    share("f2_z", "z", total("f2_xc", "xc"))
+    wait("f2_k", "k16")
+    fk = recv["f2_k"]
+    share("f2_z", "z", jnp.concatenate([jnp.sum(fk[0:8], axis=0), jnp.sum(fk[8:16], axis=0)], axis=0))
     wait("e1", "zc")
     values_on("e2", "e1", 16, 16, "k16")
     wait("r_y", "y4")
@@ -445,41 +458,39 @@
             axis=0,
         ),
     )
-    share("f2_y", "y4", total("f2_z", "z"))
     wait("c2", "k16")
     c2h = recv["c2"][:, 0:16, :].reshape(256, 128)
-    lab_in = recv["c2"][:, 16:32, :].reshape(256, 128)
-    lab_col = jnp.sum(jnp.where(iota((256, 128), 1) == k16, lab_in, 0.0), axis=1, keepdims=True)
+    lab_col = label_column(jnp.broadcast_to(recv["c2"][:, 16:17, :], (16, 16, 128)).reshape(256, 128), 0)
     oh2 = ones_where(iota((256, 128), 1).astype(jnp.float32) == lab_col - 1.0)
-    ohq2 = mm(oh2, QW3)
-    kl2 = jnp.concatenate([t_mm(c2h[0:128], ohq2[0:128]), t_mm(c2h[128:256], ohq2[128:256])], axis=0)
+    ohq2 = mm(oh2, QW3, HIGHEST)
+    kl2 = jnp.concatenate([t_mm(c2h[0:128], ohq2[0:128], HIGHEST), t_mm(c2h[128:256], ohq2[128:256], HIGHEST)], axis=0)
+    share("f2_g", "c", total("f2_z", "z"))
     wait("r_g", "xc")
     rg = recv["r_g"]
     cr2_each = [rg[:, 0:16, :].reshape(128, 128), rg[:, 16:32, :].reshape(128, 128)]
     m3 = rg[:, 32:48, :].reshape(128, 128)
-    wait("f2_y", "y4")
-    fy = recv["f2_y"]
+    wait("e2", "k16")
+    came2 = values_in("e2", 16)
+    t3_src = t3_src + mm(came2, ohq2)
+    wait("f2_g", "c")
+    fg = recv["f2_g"]
     hq2_each, w2_each = [], []
     for v in range(2):
-        t_q = fy[2 * v, 0:8, :] + fy[2 * v + 1, 0:8, :]
-        t_v = fy[2 * v, 8:16, :] + fy[2 * v + 1, 8:16, :]
+        t_q = fg[0, 8 * v : 8 * v + 8, :]
+        t_v = fg[1, 8 * v : 8 * v + 8, :]
         hq = t_q * mask_of(rnk2, v, 0)
         hq2_each.append(hq)
         w2_each.append((t_v + mm(hq, cr2_each[v])) * mask_of(rnk2, v, 1))
+    t3_w = mm(jnp.concatenate(w2_each, axis=1), kl2)
+    front2 = (iota((16, 256), 0) >> 3) == (iota((16, 256), 1) >> 7)
+    t3 = t3_src - t3_w
+    scatter_halves("f3_c", t3[:, 0:128], t3[:, 128:256])
     first = u == 0
     hq2 = jnp.where(first, hq2_each[0], hq2_each[1])
     cr2 = jnp.where(first, cr2_each[0], cr2_each[1])
     mh2, mc2 = mask_of(rnk2, u, 0), mask_of(rnk2, u, 1)
-    z2 = (loc2 + mm_t(hq2, exp2[...])) * piv2[...]
-    zp2_own = mm(z2, exp2[...])
-
-    t3_w = mm(jnp.concatenate(w2_each, axis=1), kl2)
-    front2 = (iota((16, 256), 0) >> 3) == (iota((16, 256), 1) >> 7)
-    wait("e2", "k16")
-    came2 = values_in("e2", 16)
-    t3 = t3_src + mm(came2, ohq2) - t3_w
-    scatter_halves("f3_c", t3[:, 0:128], t3[:, 128:256])
-    share("zp_xc", "xc", jnp.concatenate([zp1_own, zp2_own], axis=0))
+    z2 = (loc2 + mm_t(hq2, exp2[...], HIGHEST)) * piv2[...]
+    zp2_own = mm(z2, exp2[...], HIGHEST)
     share("f3_k", "k16", total("f3_c", "c"))
     e2 = jnp.where(front2, mm_t(jnp.concatenate(w2_each, axis=0), c2h), 0.0)
     b3 = src3[...] + mm(came2 - (e2[0:8] + e2[8:16]), oh2)
@@ -488,12 +499,13 @@
     vals = mm_t(zeta3, oh2)
     u2_own = mm(jnp.where(front2, jnp.concatenate([vals, vals], axis=0), 0.0), c2h)
     share("f3_z", "z", total("f3_k", "k16"))
-    zeta2 = mm_t(z2, blk2[...])
+    share("zp_xc", "xc", jnp.concatenate([zp1_own, zp2_own], axis=0))
+    zeta2 = mm_t(z2, blk2[...], HIGHEST)
     mh3 = mask_of(rnk3, 0, 0)
-    zp_sum = total("zp_xc", "xc")
     QW0 = chain(Q0, blk0[...], V0)
+    down1 = jnp.concatenate([t_mm(oh1[0:64], c1h[0:64]), t_mm(oh1[64:128], c1h[64:128])], axis=1)
+    ks1, kx1 = down1[0:128], down1[128:256]
     share("f3_g", "c", total("f3_z", "z"))
-    share("zp_z", "z", zp_sum)
     wait("f3_g", "c")
     hq3 = recv["f3_g"][0] * mh3
     g3 = (recv["f3_g"][1] + mm(hq3, m3)) * mh3
@@ -502,11 +514,12 @@
     u2_low = mm_t(gh3, kl2)
     scatter_halves("u2_c", u2_own[0:8] + u2_low[:, 0:128], u2_own[8:16] + u2_low[:, 128:256])
     x3 = zeta3 + mm_t(gh3, QW3)
+    values_down("g1", oh2, x3, 16, "k16")
     share("u2_k", "k16", total("u2_c", "c"))
-    values_down("g1", oh2, x3, 16, "k16")
+    share("zp_z", "z", total("zp_xc", "xc"))
     out[3] = x3
-    vals = mm_t(zeta2, oh1[:, 0:128])
-    share("x0c", "x", t_mm(exp0[...], V0))
+    u1_own = mm(zeta2, ks1)
+    share("x0c", "x", t_mm(exp0[...], V0, HIGHEST))
     share("u2_z", "z", total("u2_k", "k16"))
     wait("g1", "k16")
     values_on("g2", "g1", 16, 16, "zc")
@@ -517,38 +530,38 @@
     zp2 = total("zp_y", "y2")
     wait("g2", "zc")
     xu2 = values_back("g2", pick2, block2)
-    vals = vals + mm_t(xu2, oh1[:, 128:256])
-    u1_own = mm(jnp.where(front1, jnp.concatenate([vals, vals], axis=0), 0.0), c1h)
+    u1_own = u1_own + mm(xu2, kx1)
     wait("u2_g", "c")
     s2 = recv["u2_g"][u] * mc2
     g2 = (zp2 - mm_t(s2, cr2)) * mh2
     gs2 = jnp.concatenate([g2, -s2], axis=1)
 
     u1_low = mm_t(gs2, kl1)
-    share("u1_xc", "xc", u1_own + jnp.concatenate([u1_low[:, 0:128], u1_low[:, 128:256]], axis=0))
+    scatter_halves("u1_c", u1_own[:, 0:128] + u1_low[:, 0:128], u1_own[:, 128:256] + u1_low[:, 128:256])
     x2 = zeta2 + mm_t(gs2, QW2)
+    values_down("h1", oh1, jnp.concatenate([x2, xu2], axis=1), 8, "k8")
+    share("u1_k", "k8", total("u1_c", "c"))
     out[2] = x2
-    values_down("h1", oh1, jnp.concatenate([x2, xu2], axis=1), 8, "k8")
-    share("u1_z", "z", total("u1_xc", "xc"))
+    share("u1_z", "z", total("u1_k", "k8"))
     vals = mm_t(zeta1, oh0[:, 0:128])
     cr0 = total("x0c", "x")
     zp0 = total("zp0", "x")
-    zeta0 = mm_t(z0, blk0[...])
+    zeta0 = mm_t(z0, blk0[...], HIGHEST)
     wait("h1", "k8")
     values_on("h2", "h1", 16, 8, "zc")
-    share("u1_y", "y2", total("u1_z", "z"))
+    share("u1_g", "c", total("u1_z", "z"))
     wait("h2", "zc")
     xu1 = values_back("h2", pick1, block1)
     vals = vals + mm_t(xu1, oh0[:, 128:256])
-    s1_all = total("u1_y", "y2")
-    s1 = jnp.where(yb == 0, s1_all[0:8], s1_all[8:16]) * mc1
+    wait("u1_g", "c")
+    s1 = recv["u1_g"][yb] * mc1
     g1 = (zp1 - mm_t(s1, cr1)) * mh1
     gs1 = jnp.concatenate([g1, -s1], axis=1)
 
     vals = vals + mm_t(gs1, ohq0)
     send["u0_zc"][...] = mm(jnp.where(front0, stack16(vals), 0.0), c0h).reshape(16, 8, 128)
     start("u0_zc", "zc")
-    out[1] = zeta1 + mm_t(gs1, QW1)
+    out[1] = zeta1 + mm_t(gs1, QW1, HIGHEST)
     share("u0_x", "x", total("u0_zc", "zc"))
     s0 = total("u0_x", "x") * mc0
     g0 = (zp0 - mm_t(s0, cr0)) * mh0
@@ -597,7 +610,7 @@
         pl.pallas_call(
             apart,
             out_shape=[jax.ShapeDtypeStruct((8, 128), jnp.float32)] * 4,
-            in_specs=[hbm],
+            in_specs=[vmem],
             out_specs=[hbm] * 4,
             scratch_shapes=[pltpu.SemaphoreType.DMA((4,))],
             name="apart",

time: 98.6 us -> 96.3 us (0.977)
  Pallas kernels: 97.6 us -> 95.5 us
    pallas_call x1, Pallas kernels: 96 us -> 94.1 us  [shards(): pl.pallas_call(kernel, out_shape=jax.ShapeDtypeStruct((4, 8, 128), jnp.fl...]
where the time goes in v4:
time: 96.3 us; the launch traced here: 96.1 us
  Pallas kernels  95.5 us (99%)
    pallas_call x1, Pallas kernels, shards(): pl.pallas_call(kernel, out_shape=jax.ShapeDtypeStruct((4, 8, 128), jnp.fl...  94.1 us

profile of v4, /device:TPU:1, one launch (start us, length us, event | category | flops | bytes accessed | tf_op | source)
XLA Modules:
  0.0 96.1 jit_solution(7237051313012611060)
XLA Ops:
  0.6 94.1 %solve.1.answers = f32[4,8,128]{2,1,0:T(8,128)} custom-call(f32[8,128]{1,0:T(8,128)} %refs_0_.1, f32[128,128]{1,0:T(8,128)} %refs_1_.1, f32[128,128]{1,0:T(8,128)} %refs_2_.1, f32[128,256]{1,0:T(8,128)} %refs_3_.1, f32[1,128]{1,0:T(1,128)} %bitcast.12, f32[256,128]{1,0:T(8,128)} %refs_5_.1, s32[2,64]{1,0:T(2,128)} %bitcast.9, s32[1,256]{1,0:T(1,128)} %bitcast.10, ...), custom_call_target="tpu_custom_call" | custom-call | tf_op jit(solution)/shard_map/solve/pallas_call | solution.py:598
  94.7 1.4 %apart.1 = (f32[8,128]{1,0:T(8,128)}, f32[8,128]{1,0:T(8,128)}, f32[8,128]{1,0:T(8,128)}, f32[8,128]{1,0:T(8,128)}) custom-call(f32[4,8,128]{2,1,0:T(8,128)} %solve.1.answers), custom_call_target="tpu_custom_call" | custom-call | tf_op jit(solution)/shard_map/apart/pallas_call | solution.py:610

commit v5 on v4

--- a/solution.py
+++ b/solution.py
@@ -333,6 +333,9 @@
     t0 = mm(src0[...], Q0, HIGHEST)
     loc0 = mm(src0[...], blk0[...], HIGHEST)
 
+    cr0_own = t_mm(exp0[...], V0, HIGHEST)
+    w0_own = mm(loc0, V0, HIGHEST)
+
     pl.semaphore_wait(barrier, greeted)
     share("x0a", "x", t0)
     start("a1", "zc")
@@ -341,10 +344,9 @@
     V1 = bas1[:, 128:256]
     send["q_xc"][...] = t_mm(exp1[...], V1, HIGHEST).reshape(8, 16, 128)
     hq0 = total("x0a", "x") * mh0
-    y0 = loc0 + mm_t(hq0, exp0[...], HIGHEST)
-    share("x0b", "x", mm(y0, V0))
+    share("x0b", "x", w0_own + mm(hq0, cr0_own))
     start("q_xc", "xc")
-    z0 = y0 * piv0[...]
+    z0 = (loc0 + mm_t(hq0, exp0[...], HIGHEST)) * piv0[...]
     QW1 = chain(bas1[:, 0:128], blk1[...], V1)
     t1_src = mm(src1[...], QW1, HIGHEST)
     share("w0", "zc", total("x0b", "x") * mc0)
@@ -503,23 +505,26 @@
     zeta2 = mm_t(z2, blk2[...], HIGHEST)
     mh3 = mask_of(rnk3, 0, 0)
     QW0 = chain(Q0, blk0[...], V0)
+    m3 = m3 * mh3
+    low2 = jnp.concatenate([kl2[:, 128:256] + mm_t(kl2[:, 0:128], m3, HIGHEST), kl2[:, 0:128]], axis=1)
+    low1 = kl1[:, 128:256] + mm(kl1[:, 0:128] * mh2, cr2, HIGHEST)
+    QR2 = QW2[:, 128:256] + mm(QW2[:, 0:128] * mh2, cr2, HIGHEST)
     down1 = jnp.concatenate([t_mm(oh1[0:64], c1h[0:64]), t_mm(oh1[64:128], c1h[64:128])], axis=1)
     ks1, kx1 = down1[0:128], down1[128:256]
     share("f3_g", "c", total("f3_z", "z"))
     wait("f3_g", "c")
     hq3 = recv["f3_g"][0] * mh3
-    g3 = (recv["f3_g"][1] + mm(hq3, m3)) * mh3
-    gh3 = jnp.concatenate([g3, hq3], axis=1)
-
-    u2_low = mm_t(gh3, kl2)
+    half3 = recv["f3_g"][1] * mh3
+
+    u2_low = mm_t(jnp.concatenate([hq3, half3], axis=1), low2)
     scatter_halves("u2_c", u2_own[0:8] + u2_low[:, 0:128], u2_own[8:16] + u2_low[:, 128:256])
-    x3 = zeta3 + mm_t(gh3, QW3)
+    x3 = zeta3 + mm_t(jnp.concatenate([half3 + mm(hq3, m3), hq3], axis=1), QW3)
     values_down("g1", oh2, x3, 16, "k16")
     share("u2_k", "k16", total("u2_c", "c"))
     share("zp_z", "z", total("zp_xc", "xc"))
     out[3] = x3
     u1_own = mm(zeta2, ks1)
-    share("x0c", "x", t_mm(exp0[...], V0, HIGHEST))
+    share("x0c", "x", cr0_own)
     share("u2_z", "z", total("u2_k", "k16"))
     wait("g1", "k16")
     values_on("g2", "g1", 16, 16, "zc")
@@ -527,23 +532,27 @@
     zp1 = zp_sum[0:8]
     share("zp_y", "y2", zp_sum[8:16])
     share("u2_g", "c", total("u2_z", "z"))
-    zp2 = total("zp_y", "y2")
+    zp2 = total("zp_y", "y2") * mh2
+    u1_own = u1_own + mm_t(zp2, kl1[:, 0:128])
+    x2_own = zeta2 + mm_t(zp2, QW2[:, 0:128])
+    low0 = ohq0[:, 128:256] + mm(ohq0[:, 0:128] * mh1, cr1, HIGHEST)
+    QR1 = QW1[:, 128:256] + mm(QW1[:, 0:128] * mh1, cr1, HIGHEST)
     wait("g2", "zc")
     xu2 = values_back("g2", pick2, block2)
     u1_own = u1_own + mm(xu2, kx1)
     wait("u2_g", "c")
     s2 = recv["u2_g"][u] * mc2
-    g2 = (zp2 - mm_t(s2, cr2)) * mh2
-    gs2 = jnp.concatenate([g2, -s2], axis=1)
-
-    u1_low = mm_t(gs2, kl1)
-    scatter_halves("u1_c", u1_own[:, 0:128] + u1_low[:, 0:128], u1_own[:, 128:256] + u1_low[:, 128:256])
-    x2 = zeta2 + mm_t(gs2, QW2)
+
+    u1_own = u1_own - mm_t(s2, low1)
+    scatter_halves("u1_c", u1_own[:, 0:128], u1_own[:, 128:256])
+    x2 = x2_own - mm_t(s2, QR2)
     values_down("h1", oh1, jnp.concatenate([x2, xu2], axis=1), 8, "k8")
     share("u1_k", "k8", total("u1_c", "c"))
     out[2] = x2
     share("u1_z", "z", total("u1_k", "k8"))
-    vals = mm_t(zeta1, oh0[:, 0:128])
+    zp1 = zp1 * mh1
+    vals = mm_t(zeta1, oh0[:, 0:128]) + mm_t(zp1, ohq0[:, 0:128])
+    x1_own = zeta1 + mm_t(zp1, QW1[:, 0:128])
     cr0 = total("x0c", "x")
     zp0 = total("zp0", "x")
     zeta0 = mm_t(z0, blk0[...], HIGHEST)
@@ -555,17 +564,17 @@
     vals = vals + mm_t(xu1, oh0[:, 128:256])
     wait("u1_g", "c")
     s1 = recv["u1_g"][yb] * mc1
-    g1 = (zp1 - mm_t(s1, cr1)) * mh1
-    gs1 = jnp.concatenate([g1, -s1], axis=1)
-
-    vals = vals + mm_t(gs1, ohq0)
+
+    vals = vals - mm_t(s1, low0)
     send["u0_zc"][...] = mm(jnp.where(front0, stack16(vals), 0.0), c0h).reshape(16, 8, 128)
     start("u0_zc", "zc")
-    out[1] = zeta1 + mm_t(gs1, QW1, HIGHEST)
+    out[1] = x1_own - mm_t(s1, QR1, HIGHEST)
+    zp0 = zp0 * mh0
+    x0_own = zeta0 + mm_t(zp0, Q0, HIGHEST)
+    QR0 = QW0[:, 128:256] + mm(Q0 * mh0, cr0, HIGHEST)
     share("u0_x", "x", total("u0_zc", "zc"))
     s0 = total("u0_x", "x") * mc0
-    g0 = (zp0 - mm_t(s0, cr0)) * mh0
-    out[0] = zeta0 + mm_t(jnp.concatenate([g0, -s0], axis=1), QW0)
+    out[0] = x0_own - mm_t(s0, QR0)
 
     for name, axis in pending:
         whole(name, axis).wait_send()
@@ -602,10 +611,10 @@
         out_specs=vmem,
         scratch_shapes=scratch,
         compiler_params=pltpu.CompilerParams(
-            collective_id=0, has_side_effects=True, vmem_limit_bytes=67043328
+            collective_id=0, has_side_effects=True, vmem_limit_bytes=48 * 1024 * 1024
         ),
         name="solve",
-    )(*args)
+    )(*[pltpu.with_memory_space_constraint(a, pltpu.HBM) for a in args])
     return tuple(
         pl.pallas_call(
             apart,
@@ -613,6 +622,7 @@
             in_specs=[vmem],
             out_specs=[hbm] * 4,
             scratch_shapes=[pltpu.SemaphoreType.DMA((4,))],
+            compiler_params=pltpu.CompilerParams(vmem_limit_bytes=1024 * 1024),
             name="apart",
         )(answers)
     )

time: 96.3 us -> 93.9 us (0.975)
  Pallas kernels: 95.5 us -> 93.2 us
    pallas_call x1, Pallas kernels: 94.1 us -> 92.5 us  [shards(): pl.pallas_call(kernel, out_shape=jax.ShapeDtypeStruct((4, 8, 128), jnp.fl...]
where the time goes in v5:
time: 93.9 us; the launch traced here: 93.8 us
  Pallas kernels  93.2 us (99%)
    pallas_call x1, Pallas kernels, shards(): pl.pallas_call(kernel, out_shape=jax.ShapeDtypeStruct((4, 8, 128), jnp.fl...  92.5 us

profile of v5, /device:TPU:1, one launch (start us, length us, event | category | flops | bytes accessed | tf_op | source)
XLA Modules:
  0.0 93.8 jit_solution(18022238721639593780)
XLA Ops:
  0.6 92.5 %solve.1.answers = f32[4,8,128]{2,1,0:T(8,128)S(1)} custom-call(f32[8,128]{1,0:T(8,128)} %refs_0_.1, f32[128,128]{1,0:T(8,128)} %refs_1_.1, f32[128,128]{1,0:T(8,128)} %refs_2_.1, f32[128,256]{1,0:T(8,128)} %refs_3_.1, f32[1,128]{1,0:T(1,128)} %bitcast.12, f32[256,128]{1,0:T(8,128)} %refs_5_.1, s32[2,64]{1,0:T(2,128)} %bitcast.9, s32[1,256]{1,0:T(1,128)} %bitcast.10, ...), custom_call_target="tpu_custom_call" | custom-call | tf_op jit(solution)/shard_map/solve/pallas_call | solution.py:607
  93.2 0.6 apart.1
